TPU v7x, 32 devices: a whole 2x2x4 slice. The times are simulated.
32 devices in a mesh: ta: 4 (over z), gz: 4 (over x, core), xy: 2 (over y).
Axes of the slice: x: 2, y: 2, z: 4, core: 2. Of those that a mesh axis runs over, the one named last changes fastest.
Arguments:
- links: float32 [4, 2, 3, 3, 4, 8, 512], P(None, None, None, None, 'ta', 'xy', 'gz'), may hold values from -0.72 to 1.72
- guess: float32 [12, 2, 4, 3, 4, 8, 512], P(None, None, None, None, 'ta', 'xy', 'gz'), may hold values from -1.5 to 1.5
- source_sites: int32 [4, 2, 4, 4], P('ta', 'xy', 'gz'), may hold values from 0 to 31, as said below
Outputs:
- solution: float32 [12, 2, 4, 3, 4, 8, 512], P(None, None, None, None, 'ta', 'xy', 'gz')
- residual: float32 [12, 2, 4, 3, 4, 8, 512], P(None, None, None, None, 'ta', 'xy', 'gz')
Inputs may be any that keep to these rules, and one draw needn't show every extreme that they name: `source_sites`: each entry is an offset inside its block: time below 1, y below 4, z below 4, x below 32.
All inputs are finite; a program needn't handle non-finite values.
Results may differ from a plain program's by a relative error of at most 0.00012.
Values sent between devices are 32-bit elements; how exact they have to be, the bound alone decides.
A program may use at most 128 MiB of HBM per device.

v0:
```python
import functools

import jax
import jax.numpy as jnp
from jax import lax
from jax.experimental import pallas as pl
from jax.experimental.pallas import tpu as pltpu
from jax.sharding import PartitionSpec as P

LX = 32
NSMEAR = 8
HOP = 0.12
PAIRS = 6
EDGE_CHUNK = 3
TIME_CHUNK = 1
MESH = pl.DeviceIdType.MESH
AXES = ("xy", "gz", "ta")

E_ROWS = (
    ((1, -1j), (0, -1j)),
    ((1, -1), (0, 1)),
    ((0, -1j), (1, 1j)),
    ((0, 1), (1, 1)),
)


def times(coef, z):
    re, im = z
    if coef == 1:
        return (1, re), (1, im)
    if coef == -1:
        return (-1, re), (-1, im)
    if coef == 1j:
        return (-1, im), (1, re)
    return (1, im), (-1, re)


def add_term(z, coef, other):
    out = []
    for base, (sign, term) in zip(z, times(coef, other)):
        out.append(base + term if sign > 0 else base - term)
    return tuple(out)


def project(f, mu, parity):
    half = []
    for row in range(2):
        column, coef = E_ROWS[mu][row]
        half.append([add_term(f[row][a], parity * coef, f[2 + column][a]) for a in range(3)])
    return half


def lift_add(total, h, mu, parity):
    for row in range(2):
        column, coef = E_ROWS[mu][row]
        for a in range(3):
            total[row][a] = add_term(total[row][a], 1, h[row][a])
            low = parity * complex(coef).conjugate()
            total[2 + column][a] = add_term(total[2 + column][a], low, h[row][a])


def link_times(link, mu, vectors, adjoint):
    def entry(a, b):
        if adjoint:
            a, b = b, a
        base = mu * 18 + a * 3 + b
        return link[base], link[base + 9]

    out = [[None] * 3 for _ in vectors]
    for a in range(3):
        totals = [None] * len(vectors)
        for b in range(3):
            ur, ui = entry(a, b)
            for k, vec in enumerate(vectors):
                re, im = vec[b]
                if adjoint:
                    tr, ti = ur * re + ui * im, ur * im - ui * re
                else:
                    tr, ti = ur * re - ui * im, ur * im + ui * re
                old = totals[k]
                totals[k] = (tr, ti) if old is None else (old[0] + tr, old[1] + ti)
        for k in range(len(vectors)):
            out[k][a] = totals[k]
    return out


def flat(vectors):
    return [vec[a][part] for part in range(2) for vec in vectors for a in range(3)]


def unflat(items, count):
    return [
        [(items[k * 3 + a], items[3 * count + k * 3 + a]) for a in range(3)] for k in range(count)
    ]


class Shifts:
    def __init__(self):
        row = lax.broadcasted_iota(jnp.int32, (8, 128), 0)
        lane = lax.broadcasted_iota(jnp.int32, (8, 128), 1)
        self.low = row < 4
        self.lane = lane
        self.place = ([row % 4 == k for k in range(4)], [lane // LX == k for k in range(4)])
        self.x_first = lane % LX == 0
        self.x_last = lane % LX == LX - 1
        self.unit = ((0, 1, 8), (1, LX, 128))

    def roll(self, v, kind, steps):
        axis, unit, size = self.unit[kind]
        amount = (steps * unit) % size
        return v if amount == 0 else pltpu.roll(v, amount, axis)

    def pack(self, items, kind, ahead):
        packed = []
        for g in range(0, len(items), 4):
            out = None
            for k in range(4):
                v = self.roll(items[g + k], kind, k if ahead else k - 3)
                out = v if out is None else jnp.where(self.place[kind][k], v, out)
            packed.append(out)
        return packed

    def shift(self, items, packed, kind, ahead):
        outs = []
        for i, v in enumerate(items):
            got = packed[i // 4]
            k = i % 4
            if ahead:
                moved = self.roll(v, kind, -1)
                outs.append(jnp.where(self.place[kind][3], self.roll(got, kind, 3 - k), moved))
            else:
                moved = self.roll(v, kind, 1)
                outs.append(jnp.where(self.place[kind][0], self.roll(got, kind, -k), moved))
        return outs

    def along_x(self, items, ahead):
        outs = []
        for v in items:
            if ahead:
                a, b = pltpu.roll(v, 127, 1), pltpu.roll(v, LX - 1, 1)
                outs.append(jnp.where(self.x_last, b, a))
            else:
                a, b = pltpu.roll(v, 1, 1), pltpu.roll(v, 129 - LX, 1)
                outs.append(jnp.where(self.x_first, b, a))
        return outs


def kernel(
    sizes, sites_ref, links_ref, guess_ref, sol_ref, res_ref,
    link, guess, field_a, field_b, search, acc, right, carried,
    edge_out, edge_in, time_out, time_in, sm_out, sm_in, smt_out, smt_in,
    red_out, red_in, sums,
    edge_sem, time_sem, w_send, sm_sem, smt_sem, s_send, red_sem, r_send,
):
    n_of = dict(zip(AXES, sizes))
    me = {axis: lax.axis_index(axis) for axis in AXES}

    def peer(axis, step):
        return {axis: lax.rem(me[axis] + step + n_of[axis], n_of[axis])}

    barrier = pltpu.get_barrier_semaphore()
    for axis in AXES:
        for k in range(1, n_of[axis]):
            pl.semaphore_signal(barrier, inc=1, device_id=peer(axis, k), device_id_type=MESH)

    sh = Shifts()

    sign = jnp.where(me["ta"] == n_of["ta"] - 1, -1.0, 1.0).astype(jnp.float32)
    for i in range(72):
        v = links_ref[i]
        if i >= 54:
            v = v * sign
        link[i, 0:4, :] = v
        link[i, 4:8, :] = v

    def rhs_of(p):
        first = jnp.where(p < 4, 3 * p, 6 * p - 22)
        second = jnp.where(p < 4, 3 * p + 1, 6 * p - 19)
        return first, second

    def load_guess(p, _):
        first, second = rhs_of(p)
        for i in range(24):
            guess[p, i, 0:4, :] = guess_ref[first, i]
            guess[p, i, 4:8, :] = guess_ref[second, i]
        return _

    lax.fori_loop(0, PAIRS, load_guess, 0)
    pl.semaphore_wait(barrier, sum(n - 1 for n in sizes))

    def part_of(p, chunk):
        return pl.ds(p, chunk)

    def start_last(make, w, d, p, chunk):
        if chunk == 1:
            make(w, d, p).start()
        else:
            @pl.when(lax.rem(p, chunk) == chunk - 1)
            def _():
                make(w, d, p - (chunk - 1)).start()

    def await_first(make, w, p, chunk, dirs):
        def wait():
            for d in dirs:
                make(w, d, p).wait_recv()
        if chunk == 1:
            wait()
        else:
            pl.when(lax.rem(p, chunk) == 0)(wait)

    def edge_copy(w, d, p):
        axis, step = (("xy", -1), ("xy", 1), ("gz", -1), ("gz", 1))[d]
        return pltpu.make_async_remote_copy(
            src_ref=edge_out.at[w, d, part_of(p, EDGE_CHUNK)], dst_ref=edge_in.at[w, d, part_of(p, EDGE_CHUNK)],
            send_sem=w_send.at[w, d, p], recv_sem=edge_sem.at[w, d, p],
            device_id=peer(axis, step), device_id_type=MESH,
        )

    def time_copy(w, d, p):
        return pltpu.make_async_remote_copy(
            src_ref=time_out.at[w, d, part_of(p, TIME_CHUNK)], dst_ref=time_in.at[w, d, part_of(p, TIME_CHUNK)],
            send_sem=w_send.at[w, 4 + d, p], recv_sem=time_sem.at[w, d, p],
            device_id=peer("ta", (-1, 1)[d]), device_id_type=MESH,
        )

    def load_field(ref, p):
        return unflat([ref[p, i] for i in range(24)], 4)

    def send_body(f, w, p, par):
        for i, v in enumerate(flat(project(f, 3, -par))):
            time_out[w, 0, p, i] = v
        start_last(time_copy, w, 0, p, TIME_CHUNK)
        for i, v in enumerate(flat(link_times(link, 3, project(f, 3, par), True))):
            time_out[w, 1, p, i] = v
        start_last(time_copy, w, 1, p, TIME_CHUNK)
        for kind, mu in ((0, 1), (1, 2)):
            for i, v in enumerate(sh.pack(flat(project(f, mu, -par)), kind, True)):
                edge_out[w, 2 * kind, p, i] = v
            start_last(edge_copy, w, 2 * kind, p, EDGE_CHUNK)
            behind = flat(link_times(link, mu, project(f, mu, par), True))
            for i, v in enumerate(behind):
                carried[kind, p, i] = v
            for i, v in enumerate(sh.pack(behind, kind, False)):
                edge_out[w, 2 * kind + 1, p, i] = v
            start_last(edge_copy, w, 2 * kind + 1, p, EDGE_CHUNK)

    def interior(src, par):
        def body(p, _):
            f = load_field(src, p)
            zero = jnp.zeros((8, 128), jnp.float32)
            total = [[(zero, zero)] * 3 for _ in range(4)]
            ahead = unflat(sh.along_x(flat(project(f, 0, -par)), True), 2)
            lift_add(total, link_times(link, 0, ahead, False), 0, -par)
            behind = flat(link_times(link, 0, project(f, 0, par), True))
            lift_add(total, unflat(sh.along_x(behind, False), 2), 0, par)
            for i, v in enumerate(flat(total)):
                acc[p, i] = v
            return _
        lax.fori_loop(0, PAIRS, body, 0)

    def receive_body(src, w, p, par):
        await_first(edge_copy, w, p, EDGE_CHUNK, range(4))
        await_first(time_copy, w, p, TIME_CHUNK, range(2))
        f = load_field(src, p)
        total = load_field(acc, p)
        for kind, mu in ((0, 1), (1, 2)):
            got = [edge_in[w, 2 * kind, p, i] for i in range(3)]
            ahead = unflat(sh.shift(flat(project(f, mu, -par)), got, kind, True), 2)
            lift_add(total, link_times(link, mu, ahead, False), mu, -par)
            got = [edge_in[w, 2 * kind + 1, p, i] for i in range(3)]
            local = [carried[kind, p, i] for i in range(12)]
            lift_add(total, unflat(sh.shift(local, got, kind, False), 2), mu, par)
        ahead = unflat([time_in[w, 0, p, i] for i in range(12)], 2)
        lift_add(total, link_times(link, 3, ahead, False), 3, -par)
        lift_add(total, unflat([time_in[w, 1, p, i] for i in range(12)], 2), 3, par)
        return [a - HOP * b for a, b in zip(flat(f), flat(total))]

    def sm_copy(step, d):
        axis, hop = (("xy", -1), ("xy", 1), ("gz", -1), ("gz", 1))[d]
        return pltpu.make_async_remote_copy(
            src_ref=sm_out.at[step, d], dst_ref=sm_in.at[step, d],
            send_sem=s_send.at[step, d], recv_sem=sm_sem.at[step, d],
            device_id=peer(axis, hop), device_id_type=MESH,
        )

    def smt_copy(d):
        return pltpu.make_async_remote_copy(
            src_ref=smt_out.at[d], dst_ref=smt_in.at[d],
            send_sem=s_send.at[NSMEAR + 1, d], recv_sem=smt_sem.at[d],
            device_id=peer("ta", (-1, 1)[d]), device_id_type=MESH,
        )

    def colour_hops(items, step, beside):
        vectors = unflat(items, 2)
        behinds = []
        for kind, mu in ((0, 1), (1, 2)):
            for i, v in enumerate(sh.pack(items, kind, True)):
                sm_out[step, 2 * kind, i] = v
            sm_copy(step, 2 * kind).start()
            behind = flat(link_times(link, mu, vectors, True))
            behinds.append(behind)
            for i, v in enumerate(sh.pack(behind, kind, False)):
                sm_out[step, 2 * kind + 1, i] = v
            sm_copy(step, 2 * kind + 1).start()
        for body, first, end in beside:
            if body in (interior_guess, interior_field):
                body()
            else:
                lax.fori_loop(first, end, body, 0)
        aheads_out = [flat(link_times(link, 0, unflat(sh.along_x(items, True), 2), False))]
        behinds_out = [sh.along_x(flat(link_times(link, 0, vectors, True)), False)]
        for kind, mu in ((0, 1), (1, 2)):
            sm_copy(step, 2 * kind).wait_recv()
            got = [sm_in[step, 2 * kind, i] for i in range(3)]
            ahead = unflat(sh.shift(items, got, kind, True), 2)
            aheads_out.append(flat(link_times(link, mu, ahead, False)))
            sm_copy(step, 2 * kind + 1).wait_recv()
            got = [sm_in[step, 2 * kind + 1, i] for i in range(3)]
            behinds_out.append(sh.shift(behinds[kind], got, kind, False))
        return aheads_out, behinds_out

    def smear_step(step, items, beside):
        aheads, behinds = colour_hops(list(items), step, beside)
        out = []
        for i, v in enumerate(items):
            total = None
            for part in aheads + behinds:
                total = part[i] if total is None else total + part[i]
            out.append((v + 0.25 * total) * 0.5)
        return tuple(out)

    def start_right(items):
        for i, v in enumerate(items):
            smt_out[0, i] = v
        smt_copy(0).start()
        for i, v in enumerate(flat(link_times(link, 3, unflat(items, 2), True))):
            smt_out[1, i] = v
        smt_copy(1).start()

    def finish_right(items, beside):
        aheads, behinds = colour_hops(items, NSMEAR, beside)
        smt_copy(0).wait_recv()
        got = unflat([smt_in[0, i] for i in range(12)], 2)
        aheads.append(flat(link_times(link, 3, got, False)))
        smt_copy(1).wait_recv()
        behinds.append([smt_in[1, i] for i in range(12)])
        diag = []
        for i, v in enumerate(items):
            total = None
            for part in aheads + behinds:
                total = part[i] if total is None else total + part[i]
            diag.append(v - HOP * total)
        diag = unflat(diag, 2)
        gs = [
            unflat([-HOP * (a - b) for a, b in zip(aheads[mu], behinds[mu])], 2)
            for mu in range(4)
        ]
        zero = jnp.zeros((8, 128), jnp.float32)

        def block(s2, s, q, a):
            if s2 == s:
                return diag[q][a]
            if s2 // 2 == s // 2:
                return (zero, zero)
            out = (zero, zero)
            for mu in range(4):
                for row in range(2):
                    column, coef = E_ROWS[mu][row]
                    if s2 < 2 and row == s2 and column == s - 2:
                        out = add_term(out, coef, gs[mu][q][a])
                    if s2 >= 2 and column == s2 - 2 and row == s:
                        out = add_term(out, complex(coef).conjugate(), gs[mu][q][a])
            return out

        for s2 in range(4):
            for a in range(3):
                column = [block(s2, s, 0, a) for s in range(4)]
                lone = [block(s2, s, 1, a) for s in range(4)]
                for part in range(2):
                    i = part * 12 + s2 * 3 + a
                    for s in range(4):
                        right[s, i] = column[s][part]
                    right[4, i] = jnp.where(sh.low, lone[0][part], lone[1][part])
                    right[5, i] = jnp.where(sh.low, lone[2][part], lone[3][part])

    def first_send(p, _):
        send_body(load_field(guess, p), 0, p, 1)
        return _

    row = lax.broadcasted_iota(jnp.int32, (8, 128), 0)
    hit = (row % 4 == sites_ref[1]) & (sh.lane == sites_ref[2] * LX + sites_ref[3])
    hit = hit & (sites_ref[0] == 0)
    one = jnp.where(hit, 1.0, 0.0).astype(jnp.float32)
    zero = jnp.zeros((8, 128), jnp.float32)
    upper, lower = jnp.where(sh.low, one, 0.0), jnp.where(sh.low, 0.0, one)
    items = tuple(flat([
        [(upper, zero), (lower, zero), (zero, zero)],
        [(zero, zero), (zero, zero), (one, zero)],
    ]))

    def interior_guess():
        interior(guess, 1)

    def interior_field():
        interior(field_a, -1)

    def second(p, _):
        out = receive_body(guess, 0, p, 1)
        for i, v in enumerate(out):
            field_a[p, i] = v
        send_body(unflat(out, 4), 1, p, -1)
        return _

    def normal(p, _):
        for i, v in enumerate(receive_body(field_a, 1, p, -1)):
            search[p, i] = v
        return _

    def third(p, _):
        out = [right[p, i] - search[p, i] for i in range(24)]
        total = None
        for i, v in enumerate(out):
            search[p, i] = v
            total = v * v if total is None else total + v * v
        sums[p] = total
        send_body(unflat(out, 4), 2, p, 1)
        return _

    beside = {
        0: [(first_send, 0, 6)],
        1: [(interior_guess, 0, 0)],
        2: [(second, 0, 2)],
        3: [(second, 2, 4)],
        4: [(second, 4, 6)],
        5: [(interior_field, 0, 0)],
        6: [(normal, 0, 2)],
        7: [(normal, 2, 4)],
        8: [(normal, 4, 6)],
    }
    for step in range(NSMEAR):
        items = smear_step(step, items, beside.get(step, []))
    items = list(items)
    start_right(items)
    finish_right(items, beside[NSMEAR])

    lax.fori_loop(0, PAIRS, third, 0)
    interior(search, 1)

    def fourth(p, _):
        out = receive_body(search, 2, p, 1)
        total = None
        for i, v in enumerate(out):
            field_b[p, i] = v
            total = v * v if total is None else total + v * v
        sums[PAIRS + p] = total
        send_body(unflat(out, 4), 3, p, -1)
        return _

    lax.fori_loop(0, PAIRS, fourth, 0)

    mine = jnp.zeros((8, 128), jnp.float32)
    for k in range(2 * PAIRS):
        mine = jnp.where(sh.lane == k, jnp.sum(sums[k], axis=1, keepdims=True), mine)
    slot = 0
    done_interior = False
    for stage, axis in enumerate(AXES):
        red_out[stage] = mine
        copies = []
        for k in range(1, n_of[axis]):
            copy = pltpu.make_async_remote_copy(
                src_ref=red_out.at[stage], dst_ref=red_in.at[slot],
                send_sem=r_send.at[slot], recv_sem=red_sem.at[slot],
                device_id=peer(axis, k), device_id_type=MESH,
            )
            copy.start()
            copies.append((copy, slot))
            slot += 1
        if not done_interior:
            interior(field_b, -1)
            done_interior = True
        for copy, place in copies:
            copy.wait()
            mine = mine + red_in[place]
    top = jnp.sum(mine[0:4], axis=0, keepdims=True)
    bottom = jnp.sum(mine[4:8], axis=0, keepdims=True)
    both = jnp.where(sh.low, top, bottom)
    curvature = pltpu.roll(both, 128 - PAIRS, 1)
    steps = both / jnp.where(sh.lane < PAIRS, curvature, 1.0)

    def last(p, _):
        out = receive_body(field_b, 3, p, -1)
        length = jnp.sum(jnp.where(sh.lane == p, steps, 0.0), axis=1, keepdims=True)
        first, second_rhs = rhs_of(p)
        for i, v in enumerate(out):
            s = search[p, i]
            res = s - length * v
            sol = guess[p, i] + length * s
            res_ref[first, i] = res[0:4]
            res_ref[second_rhs, i] = res[4:8]
            sol_ref[first, i] = sol[0:4]
            sol_ref[second_rhs, i] = sol[4:8]
        return _

    lax.fori_loop(0, PAIRS, last, 0)

    def drain(w, _):
        for p in range(0, PAIRS, EDGE_CHUNK):
            for d in range(4):
                edge_copy(w, d, p).wait_send()
        for p in range(0, PAIRS, TIME_CHUNK):
            for d in range(2):
                time_copy(w, d, p).wait_send()
        return _

    lax.fori_loop(0, 4, drain, 0)

    def drain_s(step, _):
        for d in range(4):
            sm_copy(step, d).wait_send()
        return _

    lax.fori_loop(0, NSMEAR + 1, drain_s, 0)
    for d in range(2):
        smt_copy(d).wait_send()


def on_device(sizes, links, guess, source_sites):
    rows, lanes = guess.shape[-2:]
    f32 = jnp.float32
    copies = sum(n - 1 for n in sizes)
    tile = (8, lanes)
    vm = lambda *shape: pltpu.VMEM(shape + tile, f32)
    dma = lambda *shape: pltpu.SemaphoreType.DMA(shape)
    out = jax.ShapeDtypeStruct((12, 24, rows, lanes), f32)
    sol, res = pl.pallas_call(
        functools.partial(kernel, sizes),
        out_shape=(out, out),
        in_specs=[
            pl.BlockSpec(memory_space=pltpu.SMEM),
            pl.BlockSpec(memory_space=pltpu.VMEM),
            pl.BlockSpec(memory_space=pltpu.VMEM),
        ],
        out_specs=(pl.BlockSpec(memory_space=pltpu.VMEM), pl.BlockSpec(memory_space=pltpu.VMEM)),
        scratch_shapes=[
            vm(72), vm(PAIRS, 24), vm(PAIRS, 24), vm(PAIRS, 24), vm(PAIRS, 24), vm(PAIRS, 24),
            vm(PAIRS, 24), vm(2, PAIRS, 12),
            vm(4, 4, PAIRS, 3), vm(4, 4, PAIRS, 3), vm(4, 2, PAIRS, 12), vm(4, 2, PAIRS, 12),
            vm(NSMEAR + 1, 4, 3), vm(NSMEAR + 1, 4, 3), vm(2, 12), vm(2, 12),
            vm(3), vm(copies), vm(2 * PAIRS),
            dma(4, 4, PAIRS), dma(4, 2, PAIRS), dma(4, 6, PAIRS),
            dma(NSMEAR + 1, 4), dma(2), dma(NSMEAR + 2, 4), dma(copies), dma(copies),
        ],
        compiler_params=pltpu.CompilerParams(
            collective_id=0, has_side_effects=True, vmem_limit_bytes=48 * 1024 * 1024
        ),
    )(
        source_sites.reshape(4),
        links.reshape(72, rows, lanes),
        guess.reshape(12, 24, rows, lanes),
    )
    return sol.reshape(guess.shape), res.reshape(guess.shape)


def solution(mesh):
    sizes = tuple(mesh.shape[axis] for axis in AXES)
    fields = P(None, None, None, None, "ta", "xy", "gz")
    return jax.shard_map(
        functools.partial(on_device, sizes),
        mesh=mesh,
        in_specs=(fields, fields, P("ta", "xy", "gz", None)),
        out_specs=(fields, fields),
        check_vma=False,
    )
```

profile of v0, /device:TPU:0, one launch (start us, length us, event | category | flops | bytes accessed | tf_op | source)
XLA Modules:
  0.0 73.1 jit_solution(1320794182624914820)
XLA Ops:
  0.6 0.0 copy-start.2
  0.6 0.6 copy-done.2
  1.3 0.0 copy-start
  1.3 1.1 %copy-done = f32[12,2,4,3,1,4,128]{6,5,4,3,2,1,0:T(4,128)S(1)} copy-done((f32[12,2,4,3,1,4,128]{6,5,4,3,2,1,0:T(4,128)S(1)}, f32[12,2,4,3,1,4,128]{6,5,4,3,2,1,0:T(4,128)}, u32[]{:S(2)}) %copy-start) | copy-done | bytes 589848
  2.4 0.0 copy-start.1
  2.4 0.9 %copy-done.1 = f32[4,2,3,3,1,4,128]{6,5,4,3,2,1,0:T(4,128)S(1)} copy-done((f32[4,2,3,3,1,4,128]{6,5,4,3,2,1,0:T(4,128)S(1)}, f32[4,2,3,3,1,4,128]{6,5,4,3,2,1,0:T(4,128)}, u32[]{:S(2)}) %copy-start.1) | copy-done | bytes 147480
  3.3 68.2 %shard_map.50 = (f32[12,24,4,128]{3,2,1,0:T(4,128)S(1)}, f32[12,24,4,128]{3,2,1,0:T(4,128)S(1)}) custom-call(s32[4]{0:T(128)S(1)} %bitcast.13, f32[72,4,128]{2,1,0:T(4,128)S(1)} %bitcast.12, f32[12,24,4,128]{3,2,1,0:T(4,128)S(1)} %bitcast.9), custom_call_target="tpu_custom_call" | custom-call | tf_op jit(solution)/shard_map/pallas_call | solution.py:535
  71.5 0.8 %copy.9 = f32[12,2,4,3,1,4,128]{6,5,4,3,2,1,0:T(4,128)} copy(f32[12,2,4,3,1,4,128]{6,5,4,3,2,1,0:T(4,128)S(1)} %bitcast.11) | data formatting | bytes 1179648
  72.3 0.8 %copy.10 = f32[12,2,4,3,1,4,128]{6,5,4,3,2,1,0:T(4,128)} copy(f32[12,2,4,3,1,4,128]{6,5,4,3,2,1,0:T(4,128)S(1)} %bitcast.10) | data formatting | bytes 1179648
Async XLA Ops:
  0.6 0.7 copy-start.2
  1.3 1.1 %copy-start = (f32[12,2,4,3,1,4,128]{6,5,4,3,2,1,0:T(4,128)S(1)}, f32[12,2,4,3,1,4,128]{6,5,4,3,2,1,0:T(4,128)}, u32[]{:S(2)}) copy-start(f32[12,2,4,3,1,4,128]{6,5,4,3,2,1,0:T(4,128)} %param.4) | copy-start | bytes 1769476
  2.4 0.9 %copy-start.1 = (f32[4,2,3,3,1,4,128]{6,5,4,3,2,1,0:T(4,128)S(1)}, f32[4,2,3,3,1,4,128]{6,5,4,3,2,1,0:T(4,128)}, u32[]{:S(2)}) copy-start(f32[4,2,3,3,1,4,128]{6,5,4,3,2,1,0:T(4,128)} %param.3) | copy-start | bytes 442372
where the time goes:
time: 73.3 us; the launch traced here: 73.1 us
  Pallas kernels  68.2 us (93%)
  local copies, waits for them, and re-layouts  4.25 us (6%)
    pallas_call x1, Pallas kernels, on_device(): pl.pallas_call(functools.partial(kernel, sizes), out_shape=(out, out), in...  68.2 us
    unnamed x8, local copies, waits for them, and re-layouts  4.25 us

commit v1 on v0

--- a/solution.py
+++ b/solution.py
@@ -12,6 +12,7 @@
 HOP = 0.12
 PAIRS = 6
 EDGE_CHUNK = 3
+EARLY = 4
 TIME_CHUNK = 1
 MESH = pl.DeviceIdType.MESH
 AXES = ("xy", "gz", "ta")
@@ -146,12 +147,22 @@
 
 
 def kernel(
-    sizes, sites_ref, links_ref, guess_ref, sol_ref, res_ref,
+    sizes, sites_hbm, links_hbm, guess_hbm, sol_ref, res_ref,
+    sites_ref, links_ref, guess_ref,
     link, guess, field_a, field_b, search, acc, right, carried,
     edge_out, edge_in, time_out, time_in, sm_out, sm_in, smt_out, smt_in,
-    red_out, red_in, sums,
-    edge_sem, time_sem, w_send, sm_sem, smt_sem, s_send, red_sem, r_send,
+    red_out, red_in, sums, hops,
+    load_sem, edge_sem, time_sem, sm_sem, smt_sem, red_sem, send_sem,
 ):
+    loads = [
+        pltpu.make_async_copy(src, dst, load_sem.at[k])
+        for k, (src, dst) in enumerate(
+            ((links_hbm, links_ref), (sites_hbm, sites_ref), (guess_hbm, guess_ref))
+        )
+    ]
+    for load in loads:
+        load.start()
+
     n_of = dict(zip(AXES, sizes))
     me = {axis: lax.axis_index(axis) for axis in AXES}
 
@@ -165,6 +176,7 @@
 
     sh = Shifts()
 
+    loads[0].wait()
     sign = jnp.where(me["ta"] == n_of["ta"] - 1, -1.0, 1.0).astype(jnp.float32)
     for i in range(72):
         v = links_ref[i]
@@ -185,6 +197,8 @@
             guess[p, i, 4:8, :] = guess_ref[second, i]
         return _
 
+    loads[1].wait()
+    loads[2].wait()
     lax.fori_loop(0, PAIRS, load_guess, 0)
     pl.semaphore_wait(barrier, sum(n - 1 for n in sizes))
 
@@ -212,27 +226,35 @@
         axis, step = (("xy", -1), ("xy", 1), ("gz", -1), ("gz", 1))[d]
         return pltpu.make_async_remote_copy(
             src_ref=edge_out.at[w, d, part_of(p, EDGE_CHUNK)], dst_ref=edge_in.at[w, d, part_of(p, EDGE_CHUNK)],
-            send_sem=w_send.at[w, d, p], recv_sem=edge_sem.at[w, d, p],
+            send_sem=send_sem.at[0], recv_sem=edge_sem.at[lax.rem(w, 2), d, p // EDGE_CHUNK],
             device_id=peer(axis, step), device_id_type=MESH,
         )
 
     def time_copy(w, d, p):
         return pltpu.make_async_remote_copy(
             src_ref=time_out.at[w, d, part_of(p, TIME_CHUNK)], dst_ref=time_in.at[w, d, part_of(p, TIME_CHUNK)],
-            send_sem=w_send.at[w, 4 + d, p], recv_sem=time_sem.at[w, d, p],
+            send_sem=send_sem.at[1], recv_sem=time_sem.at[lax.rem(w, 2), d, p],
             device_id=peer("ta", (-1, 1)[d]), device_id_type=MESH,
         )
 
     def load_field(ref, p):
         return unflat([ref[p, i] for i in range(24)], 4)
 
-    def send_body(f, w, p, par):
+    def send_time(f, w, p, par, held=False):
+        def start(d):
+            if held:
+                pl.when(p < PAIRS - 1)(lambda: time_copy(w, d, p).start())
+            else:
+                time_copy(w, d, p).start()
+
         for i, v in enumerate(flat(project(f, 3, -par))):
             time_out[w, 0, p, i] = v
-        start_last(time_copy, w, 0, p, TIME_CHUNK)
+        start(0)
         for i, v in enumerate(flat(link_times(link, 3, project(f, 3, par), True))):
             time_out[w, 1, p, i] = v
-        start_last(time_copy, w, 1, p, TIME_CHUNK)
+        start(1)
+
+    def send_edges(f, w, p, par):
         for kind, mu in ((0, 1), (1, 2)):
             for i, v in enumerate(sh.pack(flat(project(f, mu, -par)), kind, True)):
                 edge_out[w, 2 * kind, p, i] = v
@@ -244,7 +266,7 @@
                 edge_out[w, 2 * kind + 1, p, i] = v
             start_last(edge_copy, w, 2 * kind + 1, p, EDGE_CHUNK)
 
-    def interior(src, par):
+    def interior(src, par, first=0, end=PAIRS):
         def body(p, _):
             f = load_field(src, p)
             zero = jnp.zeros((8, 128), jnp.float32)
@@ -256,7 +278,7 @@
             for i, v in enumerate(flat(total)):
                 acc[p, i] = v
             return _
-        lax.fori_loop(0, PAIRS, body, 0)
+        lax.fori_loop(first, end, body, 0)
 
     def receive_body(src, w, p, par):
         await_first(edge_copy, w, p, EDGE_CHUNK, range(4))
@@ -279,18 +301,18 @@
         axis, hop = (("xy", -1), ("xy", 1), ("gz", -1), ("gz", 1))[d]
         return pltpu.make_async_remote_copy(
             src_ref=sm_out.at[step, d], dst_ref=sm_in.at[step, d],
-            send_sem=s_send.at[step, d], recv_sem=sm_sem.at[step, d],
+            send_sem=send_sem.at[2], recv_sem=sm_sem.at[step % 2, d],
             device_id=peer(axis, hop), device_id_type=MESH,
         )
 
     def smt_copy(d):
         return pltpu.make_async_remote_copy(
             src_ref=smt_out.at[d], dst_ref=smt_in.at[d],
-            send_sem=s_send.at[NSMEAR + 1, d], recv_sem=smt_sem.at[d],
+            send_sem=send_sem.at[3], recv_sem=smt_sem.at[d],
             device_id=peer("ta", (-1, 1)[d]), device_id_type=MESH,
         )
 
-    def colour_hops(items, step, beside):
+    def colour_hops(items, step, beside, take):
         vectors = unflat(items, 2)
         behinds = []
         for kind, mu in ((0, 1), (1, 2)):
@@ -302,32 +324,31 @@
             for i, v in enumerate(sh.pack(behind, kind, False)):
                 sm_out[step, 2 * kind + 1, i] = v
             sm_copy(step, 2 * kind + 1).start()
-        for body, first, end in beside:
-            if body in (interior_guess, interior_field):
-                body()
-            else:
-                lax.fori_loop(first, end, body, 0)
-        aheads_out = [flat(link_times(link, 0, unflat(sh.along_x(items, True), 2), False))]
-        behinds_out = [sh.along_x(flat(link_times(link, 0, vectors, True)), False)]
+        beside()
+        take(
+            0,
+            flat(link_times(link, 0, unflat(sh.along_x(items, True), 2), False)),
+            sh.along_x(flat(link_times(link, 0, vectors, True)), False),
+        )
         for kind, mu in ((0, 1), (1, 2)):
             sm_copy(step, 2 * kind).wait_recv()
             got = [sm_in[step, 2 * kind, i] for i in range(3)]
             ahead = unflat(sh.shift(items, got, kind, True), 2)
-            aheads_out.append(flat(link_times(link, mu, ahead, False)))
+            ahead = flat(link_times(link, mu, ahead, False))
             sm_copy(step, 2 * kind + 1).wait_recv()
             got = [sm_in[step, 2 * kind + 1, i] for i in range(3)]
-            behinds_out.append(sh.shift(behinds[kind], got, kind, False))
-        return aheads_out, behinds_out
+            take(mu, ahead, sh.shift(behinds[kind], got, kind, False))
 
     def smear_step(step, items, beside):
-        aheads, behinds = colour_hops(list(items), step, beside)
-        out = []
-        for i, v in enumerate(items):
-            total = None
-            for part in aheads + behinds:
-                total = part[i] if total is None else total + part[i]
-            out.append((v + 0.25 * total) * 0.5)
-        return tuple(out)
+        total = [None] * 12
+
+        def take(mu, ahead, behind):
+            for i in range(12):
+                part = ahead[i] + behind[i]
+                total[i] = part if total[i] is None else total[i] + part
+
+        colour_hops(list(items), step, beside, take)
+        return tuple((v + 0.25 * t) * 0.5 for v, t in zip(items, total))
 
     def start_right(items):
         for i, v in enumerate(items):
@@ -338,38 +359,36 @@
         smt_copy(1).start()
 
     def finish_right(items, beside):
-        aheads, behinds = colour_hops(items, NSMEAR, beside)
+        def take(mu, ahead, behind):
+            for i in range(12):
+                hops[mu, i] = HOP * (behind[i] - ahead[i])
+                part = HOP * (ahead[i] + behind[i])
+                hops[4, i] = items[i] - part if mu == 0 else hops[4, i] - part
+
+        colour_hops(items, NSMEAR, beside, take)
         smt_copy(0).wait_recv()
         got = unflat([smt_in[0, i] for i in range(12)], 2)
-        aheads.append(flat(link_times(link, 3, got, False)))
+        ahead = flat(link_times(link, 3, got, False))
         smt_copy(1).wait_recv()
-        behinds.append([smt_in[1, i] for i in range(12)])
-        diag = []
-        for i, v in enumerate(items):
-            total = None
-            for part in aheads + behinds:
-                total = part[i] if total is None else total + part[i]
-            diag.append(v - HOP * total)
-        diag = unflat(diag, 2)
-        gs = [
-            unflat([-HOP * (a - b) for a, b in zip(aheads[mu], behinds[mu])], 2)
-            for mu in range(4)
-        ]
+        take(3, ahead, [smt_in[1, i] for i in range(12)])
         zero = jnp.zeros((8, 128), jnp.float32)
+
+        def pick(which, q, a):
+            return hops[which, q * 3 + a], hops[which, 6 + q * 3 + a]
 
         def block(s2, s, q, a):
             if s2 == s:
-                return diag[q][a]
+                return pick(4, q, a)
             if s2 // 2 == s // 2:
                 return (zero, zero)
-            out = (zero, zero)
+            out = None
             for mu in range(4):
                 for row in range(2):
                     column, coef = E_ROWS[mu][row]
                     if s2 < 2 and row == s2 and column == s - 2:
-                        out = add_term(out, coef, gs[mu][q][a])
+                        out = add_term(out or (zero, zero), coef, pick(mu, q, a))
                     if s2 >= 2 and column == s2 - 2 and row == s:
-                        out = add_term(out, complex(coef).conjugate(), gs[mu][q][a])
+                        out = add_term(out or (zero, zero), complex(coef).conjugate(), pick(mu, q, a))
             return out
 
         for s2 in range(4):
@@ -383,8 +402,12 @@
                     right[4, i] = jnp.where(sh.low, lone[0][part], lone[1][part])
                     right[5, i] = jnp.where(sh.low, lone[2][part], lone[3][part])
 
-    def first_send(p, _):
-        send_body(load_field(guess, p), 0, p, 1)
+    def first_time(p, _):
+        send_time(load_field(guess, p), 0, p, 1)
+        return _
+
+    def first_edges(p, _):
+        send_edges(load_field(guess, p), 0, p, 1)
         return _
 
     row = lax.broadcasted_iota(jnp.int32, (8, 128), 0)
@@ -398,52 +421,50 @@
         [(zero, zero), (zero, zero), (one, zero)],
     ]))
 
-    def interior_guess():
-        interior(guess, 1)
-
-    def interior_field():
-        interior(field_a, -1)
-
     def second(p, _):
         out = receive_body(guess, 0, p, 1)
         for i, v in enumerate(out):
             field_a[p, i] = v
-        send_body(unflat(out, 4), 1, p, -1)
-        return _
-
-    def normal(p, _):
-        for i, v in enumerate(receive_body(field_a, 1, p, -1)):
-            search[p, i] = v
+        send_time(unflat(out, 4), 1, p, -1)
+        send_edges(unflat(out, 4), 1, p, -1)
         return _
 
     def third(p, _):
-        out = [right[p, i] - search[p, i] for i in range(24)]
+        out = [right[p, i] - v for i, v in enumerate(receive_body(field_a, 1, p, -1))]
         total = None
         for i, v in enumerate(out):
             search[p, i] = v
             total = v * v if total is None else total + v * v
         sums[p] = total
-        send_body(unflat(out, 4), 2, p, 1)
-        return _
-
-    beside = {
-        0: [(first_send, 0, 6)],
-        1: [(interior_guess, 0, 0)],
-        2: [(second, 0, 2)],
-        3: [(second, 2, 4)],
-        4: [(second, 4, 6)],
-        5: [(interior_field, 0, 0)],
-        6: [(normal, 0, 2)],
-        7: [(normal, 2, 4)],
-        8: [(normal, 4, 6)],
-    }
+        send_time(unflat(out, 4), 2, p, 1)
+        send_edges(unflat(out, 4), 2, p, 1)
+        return _
+
+    def run(body, first, end):
+        lax.fori_loop(first, end, body, 0)
+
+    def beside(step):
+        if step == 0:
+            run(first_time, 0, PAIRS)
+            run(first_edges, 0, EDGE_CHUNK)
+        if step == 1:
+            run(first_edges, EDGE_CHUNK, PAIRS)
+            interior(guess, 1)
+        if 2 <= step < 2 + EARLY:
+            run(second, step - 2, step - 1)
+        if step == 2 + EARLY:
+            interior(field_a, -1, 0, EARLY)
+        if step == NSMEAR:
+            run(second, EARLY, PAIRS)
+            interior(field_a, -1, EARLY, PAIRS)
+
     for step in range(NSMEAR):
-        items = smear_step(step, items, beside.get(step, []))
+        items = smear_step(step, items, functools.partial(beside, step))
     items = list(items)
     start_right(items)
-    finish_right(items, beside[NSMEAR])
-
-    lax.fori_loop(0, PAIRS, third, 0)
+    finish_right(items, functools.partial(beside, NSMEAR))
+
+    run(third, 0, PAIRS)
     interior(search, 1)
 
     def fourth(p, _):
@@ -453,33 +474,41 @@
             field_b[p, i] = v
             total = v * v if total is None else total + v * v
         sums[PAIRS + p] = total
-        send_body(unflat(out, 4), 3, p, -1)
-        return _
-
-    lax.fori_loop(0, PAIRS, fourth, 0)
+        send_time(unflat(out, 4), 3, p, -1, held=True)
+        send_edges(unflat(out, 4), 3, p, -1)
+        return _
+
+    run(fourth, 0, PAIRS)
+
+    def normal_of(p, _):
+        for i, v in enumerate(receive_body(field_b, 3, p, -1)):
+            field_a[p, i] = v
+        return _
 
     mine = jnp.zeros((8, 128), jnp.float32)
     for k in range(2 * PAIRS):
         mine = jnp.where(sh.lane == k, jnp.sum(sums[k], axis=1, keepdims=True), mine)
     slot = 0
-    done_interior = False
     for stage, axis in enumerate(AXES):
         red_out[stage] = mine
         copies = []
         for k in range(1, n_of[axis]):
             copy = pltpu.make_async_remote_copy(
                 src_ref=red_out.at[stage], dst_ref=red_in.at[slot],
-                send_sem=r_send.at[slot], recv_sem=red_sem.at[slot],
+                send_sem=send_sem.at[4], recv_sem=red_sem.at[slot],
                 device_id=peer(axis, k), device_id_type=MESH,
             )
             copy.start()
             copies.append((copy, slot))
             slot += 1
-        if not done_interior:
+        if stage == 0:
             interior(field_b, -1)
-            done_interior = True
+        if stage == 2:
+            for d in range(2):
+                time_copy(3, d, PAIRS - 1).start()
+            run(normal_of, 0, PAIRS - 1)
         for copy, place in copies:
-            copy.wait()
+            copy.wait_recv()
             mine = mine + red_in[place]
     top = jnp.sum(mine[0:4], axis=0, keepdims=True)
     bottom = jnp.sum(mine[4:8], axis=0, keepdims=True)
@@ -488,12 +517,11 @@
     steps = both / jnp.where(sh.lane < PAIRS, curvature, 1.0)
 
     def last(p, _):
-        out = receive_body(field_b, 3, p, -1)
         length = jnp.sum(jnp.where(sh.lane == p, steps, 0.0), axis=1, keepdims=True)
         first, second_rhs = rhs_of(p)
-        for i, v in enumerate(out):
+        for i in range(24):
             s = search[p, i]
-            res = s - length * v
+            res = s - length * field_a[p, i]
             sol = guess[p, i] + length * s
             res_ref[first, i] = res[0:4]
             res_ref[second_rhs, i] = res[4:8]
@@ -501,27 +529,17 @@
             sol_ref[second_rhs, i] = sol[4:8]
         return _
 
-    lax.fori_loop(0, PAIRS, last, 0)
-
-    def drain(w, _):
-        for p in range(0, PAIRS, EDGE_CHUNK):
-            for d in range(4):
-                edge_copy(w, d, p).wait_send()
-        for p in range(0, PAIRS, TIME_CHUNK):
-            for d in range(2):
-                time_copy(w, d, p).wait_send()
-        return _
-
-    lax.fori_loop(0, 4, drain, 0)
-
-    def drain_s(step, _):
-        for d in range(4):
-            sm_copy(step, d).wait_send()
-        return _
-
-    lax.fori_loop(0, NSMEAR + 1, drain_s, 0)
-    for d in range(2):
-        smt_copy(d).wait_send()
+    run(last, 0, PAIRS - 1)
+    run(normal_of, PAIRS - 1, PAIRS)
+    run(last, PAIRS - 1, PAIRS)
+
+    for k, (sent, landed) in enumerate((
+        (edge_out, edge_in), (time_out, time_in), (sm_out, sm_in), (smt_out, smt_in), (red_in, red_in),
+    )):
+        pltpu.make_async_remote_copy(
+            src_ref=sent, dst_ref=landed, send_sem=send_sem.at[k], recv_sem=red_sem.at[0],
+            device_id=peer("ta", 1), device_id_type=MESH,
+        ).wait_send()
 
 
 def on_device(sizes, links, guess, source_sites):
@@ -536,28 +554,29 @@
         functools.partial(kernel, sizes),
         out_shape=(out, out),
         in_specs=[
-            pl.BlockSpec(memory_space=pltpu.SMEM),
-            pl.BlockSpec(memory_space=pltpu.VMEM),
-            pl.BlockSpec(memory_space=pltpu.VMEM),
+            pl.BlockSpec(memory_space=pltpu.HBM),
+            pl.BlockSpec(memory_space=pltpu.HBM),
+            pl.BlockSpec(memory_space=pltpu.HBM),
         ],
         out_specs=(pl.BlockSpec(memory_space=pltpu.VMEM), pl.BlockSpec(memory_space=pltpu.VMEM)),
         scratch_shapes=[
+            pltpu.SMEM((4,), jnp.int32), pltpu.VMEM((72, rows, lanes), f32), pltpu.VMEM((12, 24, rows, lanes), f32),
             vm(72), vm(PAIRS, 24), vm(PAIRS, 24), vm(PAIRS, 24), vm(PAIRS, 24), vm(PAIRS, 24),
             vm(PAIRS, 24), vm(2, PAIRS, 12),
             vm(4, 4, PAIRS, 3), vm(4, 4, PAIRS, 3), vm(4, 2, PAIRS, 12), vm(4, 2, PAIRS, 12),
             vm(NSMEAR + 1, 4, 3), vm(NSMEAR + 1, 4, 3), vm(2, 12), vm(2, 12),
-            vm(3), vm(copies), vm(2 * PAIRS),
-            dma(4, 4, PAIRS), dma(4, 2, PAIRS), dma(4, 6, PAIRS),
-            dma(NSMEAR + 1, 4), dma(2), dma(NSMEAR + 2, 4), dma(copies), dma(copies),
+            vm(3), vm(copies), vm(2 * PAIRS), vm(5, 12),
+            dma(3), dma(2, 4, PAIRS // EDGE_CHUNK), dma(2, 2, PAIRS), dma(2, 4), dma(2), dma(copies), dma(5),
         ],
         compiler_params=pltpu.CompilerParams(
             collective_id=0, has_side_effects=True, vmem_limit_bytes=48 * 1024 * 1024
         ),
-    )(
-        source_sites.reshape(4),
-        links.reshape(72, rows, lanes),
-        guess.reshape(12, 24, rows, lanes),
-    )
+    )(*(
+        pltpu.with_memory_space_constraint(x, pltpu.HBM)
+        for x in (
+            source_sites.reshape(4), links.reshape(72, rows, lanes), guess.reshape(12, 24, rows, lanes)
+        )
+    ))
     return sol.reshape(guess.shape), res.reshape(guess.shape)
 
 

time: 73.3 us -> 67.5 us (0.921)
  Pallas kernels: 68.2 us -> 65.1 us
  local copies, waits for them, and re-layouts: 4.25 us -> 1.63 us
    pallas_call x1, Pallas kernels: 68.2 us -> 65.1 us  [on_device(): pl.pallas_call(functools.partial(kernel, sizes), out_shape=(out, out), in...]
    unnamed x8 -> x2, local copies, waits for them, and re-layouts: 4.25 us -> 1.63 us
where the time goes in v1:
time: 67.5 us; the launch traced here: 67.4 us
  Pallas kernels  65.1 us (96%)
  local copies, waits for them, and re-layouts  1.63 us (2%)
    pallas_call x1, Pallas kernels, on_device(): pl.pallas_call(functools.partial(kernel, sizes), out_shape=(out, out), in...  65.1 us
    unnamed x2, local copies, waits for them, and re-layouts  1.63 us

profile of v1, /device:TPU:0, one launch (start us, length us, event | category | flops | bytes accessed | tf_op | source)
XLA Modules:
  0.0 67.4 jit_solution(7206961592381465008)
XLA Ops:
  0.6 65.1 %shard_map.50 = (f32[12,24,4,128]{3,2,1,0:T(4,128)S(1)}, f32[12,24,4,128]{3,2,1,0:T(4,128)S(1)}) custom-call(s32[4]{0:T(128)} %bitcast.13, f32[72,4,128]{2,1,0:T(4,128)} %bitcast.12, f32[12,24,4,128]{3,2,1,0:T(4,128)} %bitcast.11), custom_call_target="tpu_custom_call" | custom-call | tf_op jit(solution)/shard_map/pallas_call | solution.py:553
  65.7 0.8 %copy.9 = f32[12,2,4,3,1,4,128]{6,5,4,3,2,1,0:T(4,128)} copy(f32[12,2,4,3,1,4,128]{6,5,4,3,2,1,0:T(4,128)S(1)} %bitcast.10) | data formatting | bytes 1179648
  66.5 0.8 %copy.10 = f32[12,2,4,3,1,4,128]{6,5,4,3,2,1,0:T(4,128)} copy(f32[12,2,4,3,1,4,128]{6,5,4,3,2,1,0:T(4,128)S(1)} %bitcast.9) | data formatting | bytes 1179648

commit v2 on v1

--- a/solution.py
+++ b/solution.py
@@ -12,7 +12,6 @@
 HOP = 0.12
 PAIRS = 6
 EDGE_CHUNK = 3
-EARLY = 4
 TIME_CHUNK = 1
 MESH = pl.DeviceIdType.MESH
 AXES = ("xy", "gz", "ta")
@@ -100,6 +99,7 @@
         row = lax.broadcasted_iota(jnp.int32, (8, 128), 0)
         lane = lax.broadcasted_iota(jnp.int32, (8, 128), 1)
         self.low = row < 4
+        self.row = row
         self.lane = lane
         self.place = ([row % 4 == k for k in range(4)], [lane // LX == k for k in range(4)])
         self.x_first = lane % LX == 0
@@ -147,34 +147,56 @@
 
 
 def kernel(
-    sizes, sites_hbm, links_hbm, guess_hbm, sol_ref, res_ref,
-    sites_ref, links_ref, guess_ref,
+    sizes, sites_hbm, links_hbm, guess_hbm, search_ref, normal_ref, length_ref,
+    sites_ref, links_ref, guess_ref, blocks, wide, smear, carry,
     link, guess, field_a, field_b, search, acc, right, carried,
-    edge_out, edge_in, time_out, time_in, sm_out, sm_in, smt_out, smt_in,
+    edge_out, edge_in, time_out, time_in, smt_out, smt_in,
     red_out, red_in, sums, hops,
-    load_sem, edge_sem, time_sem, sm_sem, smt_sem, red_sem, send_sem,
+    load_sem, edge_sem, time_sem, block_sem, smt_sem, red_sem, send_sem,
 ):
+    n_of = dict(zip(AXES, sizes))
+    me = {axis: lax.axis_index(axis) for axis in AXES}
+    n_gz = n_of["gz"]
+    reach = min(n_of["xy"], 8)
+    own = 0 if reach == n_of["xy"] else reach // 2
+    groups = reach // 2
+
     loads = [
         pltpu.make_async_copy(src, dst, load_sem.at[k])
-        for k, (src, dst) in enumerate(
-            ((links_hbm, links_ref), (sites_hbm, sites_ref), (guess_hbm, guess_ref))
-        )
+        for k, (src, dst) in enumerate((
+            (links_hbm, links_ref), (sites_hbm, sites_ref), (guess_hbm, guess_ref),
+            (links_hbm.at[pl.ds(0, 54)], blocks.at[own * n_gz + me["gz"], pl.ds(1, 54)]),
+        ))
     ]
-    for load in loads:
-        load.start()
-
-    n_of = dict(zip(AXES, sizes))
-    me = {axis: lax.axis_index(axis) for axis in AXES}
+    for k in (3, 1, 0, 2):
+        loads[k].start()
 
     def peer(axis, step):
         return {axis: lax.rem(me[axis] + step + n_of[axis], n_of[axis])}
 
+    def across(xy, gz):
+        return {
+            "xy": lax.rem(me["xy"] + xy + n_of["xy"], n_of["xy"]),
+            "gz": lax.rem(me["gz"] + gz + n_gz, n_gz),
+        }
+
+    shifts = sorted({(slot - own) % n_of["xy"] for slot in range(reach)} | {(own - slot) % n_of["xy"] for slot in range(reach)})
+    greeted = [across(y, z) for y in shifts for z in range(n_gz) if (y, z) != (0, 0)]
+    greeted += [peer("xy", y) for y in range(1, n_of["xy"]) if y not in shifts]
+    greeted += [peer("ta", t) for t in range(1, n_of["ta"])]
     barrier = pltpu.get_barrier_semaphore()
-    for axis in AXES:
-        for k in range(1, n_of[axis]):
-            pl.semaphore_signal(barrier, inc=1, device_id=peer(axis, k), device_id_type=MESH)
+    for device in greeted:
+        pl.semaphore_signal(barrier, inc=1, device_id=device, device_id_type=MESH)
 
     sh = Shifts()
+
+    row = lax.broadcasted_iota(jnp.int32, (4, 128), 0)
+    lane = lax.broadcasted_iota(jnp.int32, (4, 128), 1)
+    loads[3].wait()
+    loads[1].wait()
+    hit = (row == sites_ref[1]) & (lane == sites_ref[2] * LX + sites_ref[3])
+    hit = hit & (sites_ref[0] == 0)
+    blocks[own * n_gz + me["gz"], 0] = jnp.where(hit, 1.0, 0.0).astype(jnp.float32)
 
     loads[0].wait()
     sign = jnp.where(me["ta"] == n_of["ta"] - 1, -1.0, 1.0).astype(jnp.float32)
@@ -197,10 +219,9 @@
             guess[p, i, 4:8, :] = guess_ref[second, i]
         return _
 
-    loads[1].wait()
     loads[2].wait()
     lax.fori_loop(0, PAIRS, load_guess, 0)
-    pl.semaphore_wait(barrier, sum(n - 1 for n in sizes))
+    pl.semaphore_wait(barrier, len(greeted))
 
     def part_of(p, chunk):
         return pl.ds(p, chunk)
@@ -297,13 +318,31 @@
         lift_add(total, unflat([time_in[w, 1, p, i] for i in range(12)], 2), 3, par)
         return [a - HOP * b for a, b in zip(flat(f), flat(total))]
 
-    def sm_copy(step, d):
-        axis, hop = (("xy", -1), ("xy", 1), ("gz", -1), ("gz", 1))[d]
+    def block_copy(slot, gz, device, to):
         return pltpu.make_async_remote_copy(
-            src_ref=sm_out.at[step, d], dst_ref=sm_in.at[step, d],
-            send_sem=send_sem.at[2], recv_sem=sm_sem.at[step % 2, d],
-            device_id=peer(axis, hop), device_id_type=MESH,
+            src_ref=blocks.at[slot * n_gz + gz], dst_ref=blocks.at[to * n_gz + gz],
+            send_sem=send_sem.at[2], recv_sem=block_sem.at[to * n_gz + gz],
+            device_id=device, device_id_type=MESH,
         )
+
+    mate = 1 - 2 * lax.rem(me["gz"], 2)
+    direct = [(slot, z) for z in range(0, n_gz, 2) for slot in range(reach) if (slot, z) != (own, 0)]
+
+    def send_blocks():
+        block_copy(own, me["gz"], across(0, mate), own).start()
+        for slot, z in direct:
+            block_copy(own, me["gz"], across(own - slot, z), slot).start()
+
+    def pass_blocks():
+        for slot, z in direct:
+            copy = block_copy(slot, lax.rem(me["gz"] - z + n_gz, n_gz), across(0, mate), slot)
+            copy.wait_recv()
+            copy.start()
+
+    def await_blocks():
+        for z in range(0, n_gz, 2):
+            for slot in range(reach):
+                block_copy(slot, lax.rem(me["gz"] + mate - z + 2 * n_gz, n_gz), across(0, mate), slot).wait_recv()
 
     def smt_copy(d):
         return pltpu.make_async_remote_copy(
@@ -312,43 +351,98 @@
             device_id=peer("ta", (-1, 1)[d]), device_id_type=MESH,
         )
 
-    def colour_hops(items, step, beside, take):
-        vectors = unflat(items, 2)
-        behinds = []
-        for kind, mu in ((0, 1), (1, 2)):
-            for i, v in enumerate(sh.pack(items, kind, True)):
-                sm_out[step, 2 * kind, i] = v
-            sm_copy(step, 2 * kind).start()
-            behind = flat(link_times(link, mu, vectors, True))
-            behinds.append(behind)
-            for i, v in enumerate(sh.pack(behind, kind, False)):
-                sm_out[step, 2 * kind + 1, i] = v
-            sm_copy(step, 2 * kind + 1).start()
-        beside()
-        take(
-            0,
-            flat(link_times(link, 0, unflat(sh.along_x(items, True), 2), False)),
-            sh.along_x(flat(link_times(link, 0, vectors, True)), False),
-        )
-        for kind, mu in ((0, 1), (1, 2)):
-            sm_copy(step, 2 * kind).wait_recv()
-            got = [sm_in[step, 2 * kind, i] for i in range(3)]
-            ahead = unflat(sh.shift(items, got, kind, True), 2)
-            ahead = flat(link_times(link, mu, ahead, False))
-            sm_copy(step, 2 * kind + 1).wait_recv()
-            got = [sm_in[step, 2 * kind + 1, i] for i in range(3)]
-            take(mu, ahead, sh.shift(behinds[kind], got, kind, False))
-
-    def smear_step(step, items, beside):
-        total = [None] * 12
-
-        def take(mu, ahead, behind):
-            for i in range(12):
-                part = ahead[i] + behind[i]
-                total[i] = part if total[i] is None else total[i] + part
-
-        colour_hops(list(items), step, beside, take)
-        return tuple((v + 0.25 * t) * 0.5 for v, t in zip(items, total))
+    def widen(z, _):
+        zero = jnp.zeros((8, 128), jnp.float32)
+        for g in range(groups):
+            for i in range(55):
+                wide[g, z, i, 0:4] = blocks[2 * g * n_gz + z, i]
+                wide[g, z, i, 4:8] = blocks[(2 * g + 1) * n_gz + z, i]
+            for c in range(3):
+                for i in range(6):
+                    smear[0, g, z, c * 6 + i] = wide[g, z, 0] if i == c else zero
+            carry_hops(0, g, z)
+        return _
+
+    def links_of(g, z):
+        return wide.at[g, z, pl.ds(1, 54)]
+
+    def colour(ref, now, g, z, c):
+        return [ref[now, g, z, c * 6 + i] for i in range(6)]
+
+    def carry_hops(now, g, z):
+        for c in range(3):
+            vector = unflat(colour(smear, now, g, z, c), 1)
+            for mu in (2,) if groups == 1 else (2, 1):
+                for i, v in enumerate(flat(link_times(links_of(g, z), mu, vector, True))):
+                    carry[2 - mu, now, g, z, c * 6 + i] = v
+
+    def beyond(items, others, kind, ahead):
+        outs = []
+        for v, other in zip(items, others):
+            step = -1 if ahead else 1
+            inner = (sh.row if kind == 0 else sh.lane // LX)
+            last = inner == ((7, 3)[kind] if ahead else 0)
+            moved = sh.roll(v, kind, step)
+            outs.append(moved if other is None else jnp.where(last, sh.roll(other, kind, step), moved))
+        return outs
+
+    def colour_hops(now, g, z, c):
+        link_at = links_of(g, z)
+        items = colour(smear, now, g, z, c)
+        vector = unflat(items, 1)
+        out = [(
+            flat(link_times(link_at, 0, unflat(sh.along_x(items, True), 1), False)),
+            sh.along_x(flat(link_times(link_at, 0, vector, True)), False),
+        )]
+        if groups == 1:
+            later, behind, before = [None] * 6, flat(link_times(link_at, 1, vector, True)), [None] * 6
+        else:
+            later = colour(smear, now, (g + 1) % groups, z, c)
+            behind = colour(carry.at[1], now, g, z, c)
+            before = colour(carry.at[1], now, (g - 1) % groups, z, c)
+        out.append((
+            flat(link_times(link_at, 1, unflat(beyond(items, later, 0, True), 1), False)),
+            beyond(behind, before, 0, False),
+        ))
+        later = colour(smear, now, g, lax.rem(z + 1, n_gz), c)
+        behind = colour(carry.at[0], now, g, z, c)
+        before = colour(carry.at[0], now, g, lax.rem(z + n_gz - 1, n_gz), c)
+        out.append((
+            flat(link_times(link_at, 2, unflat(beyond(items, later, 1, True), 1), False)),
+            beyond(behind, before, 1, False),
+        ))
+        return items, out
+
+    def smear_steps(first, end):
+        for step in range(first, end):
+            now, then = step % 2, (step + 1) % 2
+            deep = min(-(-(NSMEAR - step) // (128 // LX)), n_gz // 2)
+
+            def body(k, _):
+                z = lax.rem(me["gz"] - deep + k + n_gz, n_gz)
+                for g in range(groups):
+                    for c in range(3):
+                        items, parts = colour_hops(now, g, z, c)
+                        for i, v in enumerate(items):
+                            total = None
+                            for ahead, behind in parts:
+                                part = ahead[i] + behind[i]
+                                total = part if total is None else total + part
+                            smear[then, g, z, c * 6 + i] = (v + 0.25 * total) * 0.5
+                    carry_hops(then, g, z)
+                return _
+
+            lax.fori_loop(0, min(2 * deep + 1, n_gz), body, 0)
+
+    def paired(colours):
+        out = []
+        for part in range(2):
+            for q in range(2):
+                for a in range(3):
+                    i = part * 3 + a
+                    up, down = colours[2 * q][i], colours[1 + q][i]
+                    out.append(jnp.where(sh.low, up, pltpu.roll(down, 4, 0)))
+        return out
 
     def start_right(items):
         for i, v in enumerate(items):
@@ -358,19 +452,23 @@
             smt_out[1, i] = v
         smt_copy(1).start()
 
-    def finish_right(items, beside):
-        def take(mu, ahead, behind):
-            for i in range(12):
-                hops[mu, i] = HOP * (behind[i] - ahead[i])
-                part = HOP * (ahead[i] + behind[i])
-                hops[4, i] = items[i] - part if mu == 0 else hops[4, i] - part
-
-        colour_hops(items, NSMEAR, beside, take)
+    def local_right(items):
+        done = [colour_hops(NSMEAR % 2, own // 2, me["gz"], c)[1] for c in range(3)]
+        for mu in range(3):
+            take(mu, items, *(paired([parts[mu][side] for parts in done]) for side in range(2)))
+
+    def take(mu, items, ahead, behind):
+        for i in range(12):
+            hops[mu, i] = HOP * (behind[i] - ahead[i])
+            part = HOP * (ahead[i] + behind[i])
+            hops[4, i] = items[i] - part if mu == 0 else hops[4, i] - part
+
+    def finish_right():
         smt_copy(0).wait_recv()
         got = unflat([smt_in[0, i] for i in range(12)], 2)
         ahead = flat(link_times(link, 3, got, False))
         smt_copy(1).wait_recv()
-        take(3, ahead, [smt_in[1, i] for i in range(12)])
+        take(3, None, ahead, [smt_in[1, i] for i in range(12)])
         zero = jnp.zeros((8, 128), jnp.float32)
 
         def pick(which, q, a):
@@ -410,16 +508,11 @@
         send_edges(load_field(guess, p), 0, p, 1)
         return _
 
-    row = lax.broadcasted_iota(jnp.int32, (8, 128), 0)
-    hit = (row % 4 == sites_ref[1]) & (sh.lane == sites_ref[2] * LX + sites_ref[3])
-    hit = hit & (sites_ref[0] == 0)
-    one = jnp.where(hit, 1.0, 0.0).astype(jnp.float32)
-    zero = jnp.zeros((8, 128), jnp.float32)
-    upper, lower = jnp.where(sh.low, one, 0.0), jnp.where(sh.low, 0.0, one)
-    items = tuple(flat([
-        [(upper, zero), (lower, zero), (zero, zero)],
-        [(zero, zero), (zero, zero), (one, zero)],
-    ]))
+    def give(ref, p, out):
+        first, second_rhs = rhs_of(p)
+        for i, v in enumerate(out):
+            ref[first, i] = v[0:4]
+            ref[second_rhs, i] = v[4:8]
 
     def second(p, _):
         out = receive_body(guess, 0, p, 1)
@@ -436,6 +529,7 @@
             search[p, i] = v
             total = v * v if total is None else total + v * v
         sums[p] = total
+        give(search_ref, p, out)
         send_time(unflat(out, 4), 2, p, 1)
         send_edges(unflat(out, 4), 2, p, 1)
         return _
@@ -443,26 +537,23 @@
     def run(body, first, end):
         lax.fori_loop(first, end, body, 0)
 
-    def beside(step):
-        if step == 0:
-            run(first_time, 0, PAIRS)
-            run(first_edges, 0, EDGE_CHUNK)
-        if step == 1:
-            run(first_edges, EDGE_CHUNK, PAIRS)
-            interior(guess, 1)
-        if 2 <= step < 2 + EARLY:
-            run(second, step - 2, step - 1)
-        if step == 2 + EARLY:
-            interior(field_a, -1, 0, EARLY)
-        if step == NSMEAR:
-            run(second, EARLY, PAIRS)
-            interior(field_a, -1, EARLY, PAIRS)
-
-    for step in range(NSMEAR):
-        items = smear_step(step, items, functools.partial(beside, step))
-    items = list(items)
+    send_blocks()
+    run(first_time, 0, PAIRS)
+    run(first_edges, 0, PAIRS)
+    interior(guess, 1)
+    pass_blocks()
+    run(second, 0, 2)
+    await_blocks()
+    lax.fori_loop(0, n_gz, widen, 0)
+    smear_steps(0, 3)
+    run(second, 2, 3)
+    smear_steps(3, NSMEAR)
+    items = paired([colour(smear, NSMEAR % 2, own // 2, me["gz"], c) for c in range(3)])
     start_right(items)
-    finish_right(items, functools.partial(beside, NSMEAR))
+    run(second, 3, PAIRS)
+    local_right(items)
+    interior(field_a, -1)
+    finish_right()
 
     run(third, 0, PAIRS)
     interior(search, 1)
@@ -481,8 +572,7 @@
     run(fourth, 0, PAIRS)
 
     def normal_of(p, _):
-        for i, v in enumerate(receive_body(field_b, 3, p, -1)):
-            field_a[p, i] = v
+        give(normal_ref, p, receive_body(field_b, 3, p, -1))
         return _
 
     mine = jnp.zeros((8, 128), jnp.float32)
@@ -516,25 +606,16 @@
     curvature = pltpu.roll(both, 128 - PAIRS, 1)
     steps = both / jnp.where(sh.lane < PAIRS, curvature, 1.0)
 
-    def last(p, _):
+    run(normal_of, PAIRS - 1, PAIRS)
+    for p in range(PAIRS):
         length = jnp.sum(jnp.where(sh.lane == p, steps, 0.0), axis=1, keepdims=True)
-        first, second_rhs = rhs_of(p)
-        for i in range(24):
-            s = search[p, i]
-            res = s - length * field_a[p, i]
-            sol = guess[p, i] + length * s
-            res_ref[first, i] = res[0:4]
-            res_ref[second_rhs, i] = res[4:8]
-            sol_ref[first, i] = sol[0:4]
-            sol_ref[second_rhs, i] = sol[4:8]
-        return _
-
-    run(last, 0, PAIRS - 1)
-    run(normal_of, PAIRS - 1, PAIRS)
-    run(last, PAIRS - 1, PAIRS)
-
+        first, second_rhs = (3 * p, 3 * p + 1) if p < 4 else (6 * p - 22, 6 * p - 19)
+        length_ref[first : first + 1] = jnp.broadcast_to(length[0:1], (1, 128))
+        length_ref[second_rhs : second_rhs + 1] = jnp.broadcast_to(length[4:5], (1, 128))
+
+    passed = blocks.at[pl.ds(0, reach * n_gz - 1)]
     for k, (sent, landed) in enumerate((
-        (edge_out, edge_in), (time_out, time_in), (sm_out, sm_in), (smt_out, smt_in), (red_in, red_in),
+        (edge_out, edge_in), (time_out, time_in), (passed, passed), (smt_out, smt_in), (red_in, red_in),
     )):
         pltpu.make_async_remote_copy(
             src_ref=sent, dst_ref=landed, send_sem=send_sem.at[k], recv_sem=red_sem.at[0],
@@ -546,27 +627,32 @@
     rows, lanes = guess.shape[-2:]
     f32 = jnp.float32
     copies = sum(n - 1 for n in sizes)
+    n_gz = sizes[AXES.index("gz")]
+    reach = min(sizes[0], 8)
+    groups = reach // 2
     tile = (8, lanes)
     vm = lambda *shape: pltpu.VMEM(shape + tile, f32)
     dma = lambda *shape: pltpu.SemaphoreType.DMA(shape)
     out = jax.ShapeDtypeStruct((12, 24, rows, lanes), f32)
-    sol, res = pl.pallas_call(
+    search, normal, length = pl.pallas_call(
         functools.partial(kernel, sizes),
-        out_shape=(out, out),
+        out_shape=(out, out, jax.ShapeDtypeStruct((12, lanes), f32)),
         in_specs=[
             pl.BlockSpec(memory_space=pltpu.HBM),
             pl.BlockSpec(memory_space=pltpu.HBM),
             pl.BlockSpec(memory_space=pltpu.HBM),
         ],
-        out_specs=(pl.BlockSpec(memory_space=pltpu.VMEM), pl.BlockSpec(memory_space=pltpu.VMEM)),
+        out_specs=(pl.BlockSpec(memory_space=pltpu.VMEM),) * 3,
         scratch_shapes=[
             pltpu.SMEM((4,), jnp.int32), pltpu.VMEM((72, rows, lanes), f32), pltpu.VMEM((12, 24, rows, lanes), f32),
+            pltpu.VMEM((reach * n_gz, 55, rows, lanes), f32), vm(groups, n_gz, 55),
+            vm(2, groups, n_gz, 18), vm(min(groups, 2), 2, groups, n_gz, 18),
             vm(72), vm(PAIRS, 24), vm(PAIRS, 24), vm(PAIRS, 24), vm(PAIRS, 24), vm(PAIRS, 24),
             vm(PAIRS, 24), vm(2, PAIRS, 12),
             vm(4, 4, PAIRS, 3), vm(4, 4, PAIRS, 3), vm(4, 2, PAIRS, 12), vm(4, 2, PAIRS, 12),
-            vm(NSMEAR + 1, 4, 3), vm(NSMEAR + 1, 4, 3), vm(2, 12), vm(2, 12),
+            vm(2, 12), vm(2, 12),
             vm(3), vm(copies), vm(2 * PAIRS), vm(5, 12),
-            dma(3), dma(2, 4, PAIRS // EDGE_CHUNK), dma(2, 2, PAIRS), dma(2, 4), dma(2), dma(copies), dma(5),
+            dma(4), dma(2, 4, PAIRS // EDGE_CHUNK), dma(2, 2, PAIRS), dma(reach * n_gz), dma(2), dma(copies), dma(5),
         ],
         compiler_params=pltpu.CompilerParams(
             collective_id=0, has_side_effects=True, vmem_limit_bytes=48 * 1024 * 1024
@@ -577,6 +663,9 @@
             source_sites.reshape(4), links.reshape(72, rows, lanes), guess.reshape(12, 24, rows, lanes)
         )
     ))
+    length = length[:, None, None]
+    sol = guess.reshape(search.shape) + length * search
+    res = search - length * normal
     return sol.reshape(guess.shape), res.reshape(guess.shape)
 
 

time: 67.5 us -> 64.4 us (0.954)
  Pallas kernels: 65.1 us -> 62.3 us
  local copies, waits for them, and re-layouts: 1.63 us -> 0.01 us
  other arithmetic: 0 us -> 1.31 us
    pallas_call x1, Pallas kernels: 65.1 us -> 62.3 us  [on_device(): pl.pallas_call(functools.partial(kernel, sizes), out_shape=(out, out, jax...]
    unnamed x2, local copies, waits for them, and re-layouts: 1.63 us -> 0.01 us
    sub x0 -> x1, other arithmetic: none -> 1.31 us  [on_device(): res = search - length * normal]
where the time goes in v2:
time: 64.4 us; the launch traced here: 64.2 us
  Pallas kernels  62.3 us (97%)
  other arithmetic  1.31 us (2%)
  between operations  0.65 us (1%)
    pallas_call x1, Pallas kernels, on_device(): pl.pallas_call(functools.partial(kernel, sizes), out_shape=(out, out, jax...  62.3 us
    sub x1, other arithmetic, on_device(): res = search - length * normal  1.31 us

profile of v2, /device:TPU:0, one launch (start us, length us, event | category | flops | bytes accessed | tf_op | source)
XLA Modules:
  0.0 64.2 jit_solution(9916793473768345001)
XLA Ops:
  0.6 0.0 copy-start
  0.6 62.3 %shard_map.50 = (f32[12,24,4,128]{3,2,1,0:T(4,128)S(1)}, f32[12,24,4,128]{3,2,1,0:T(4,128)S(1)}, f32[12,128]{1,0:T(8,128)S(1)}) custom-call(s32[4]{0:T(128)} %bitcast.14, f32[72,4,128]{2,1,0:T(4,128)} %bitcast.13, f32[12,24,4,128]{3,2,1,0:T(4,128)} %bitcast.9), custom_call_target="tpu_custom_call" | custom-call | tf_op jit(solution)/shard_map/pallas_call | solution.py:637
  62.9 0.0 copy-done
  62.9 1.3 %multiply_subtract_fusion = (f32[12,24,4,128]{3,2,1,0:T(4,128)}, f32[12,24,4,128]{3,2,1,0:T(4,128)}) fusion(f32[12,24,4,128]{3,2,1,0:T(4,128)S(1)} %get-tuple-element.6, f32[12,24,4,128]{3,2,1,0:T(4,128)S(1)} %get-tuple-element.7, f32[12,128]{1,0:T(8,128)S(1)} %get-tuple-element.5, f32[12,24,4,128]{3,2,1,0:T(4,128)S(1)} %bitcast.10), kind=kLoop, calls=%fused_computation | loop fusion | flops 589824 | bytes 2955264 | tf_op jit(solution)/shard_map/sub | solution.py:668
Async XLA Ops:
  0.6 62.3 %copy-start = (f32[12,2,4,3,1,4,128]{6,5,4,3,2,1,0:T(4,128)S(1)}, f32[12,2,4,3,1,4,128]{6,5,4,3,2,1,0:T(4,128)}, u32[]{:S(2)}) copy-start(f32[12,2,4,3,1,4,128]{6,5,4,3,2,1,0:T(4,128)} %param.4) | copy-start | bytes 1769476

commit v3 on v2

--- a/solution.py
+++ b/solution.py
@@ -151,7 +151,7 @@
     sites_ref, links_ref, guess_ref, blocks, wide, smear, carry,
     link, guess, field_a, field_b, search, acc, right, carried,
     edge_out, edge_in, time_out, time_in, smt_out, smt_in,
-    red_out, red_in, sums, hops,
+    red_out, red_in, sums, hops, sources,
     load_sem, edge_sem, time_sem, block_sem, smt_sem, red_sem, send_sem,
 ):
     n_of = dict(zip(AXES, sizes))
@@ -200,17 +200,20 @@
 
     loads[0].wait()
     sign = jnp.where(me["ta"] == n_of["ta"] - 1, -1.0, 1.0).astype(jnp.float32)
-    for i in range(72):
-        v = links_ref[i]
-        if i >= 54:
-            v = v * sign
-        link[i, 0:4, :] = v
-        link[i, 4:8, :] = v
+
+    def double_links(first, end):
+        for i in range(first, end):
+            v = links_ref[i]
+            if i >= 54:
+                v = v * sign
+            link[i, 0:4, :] = v
+            link[i, 4:8, :] = v
+
+    double_links(54, 72)
 
     def rhs_of(p):
-        first = jnp.where(p < 4, 3 * p, 6 * p - 22)
-        second = jnp.where(p < 4, 3 * p + 1, 6 * p - 19)
-        return first, second
+        first = 6 * lax.rem(p, 2) + p // 2
+        return first, first + 3
 
     def load_guess(p, _):
         first, second = rhs_of(p)
@@ -220,7 +223,6 @@
         return _
 
     loads[2].wait()
-    lax.fori_loop(0, PAIRS, load_guess, 0)
     pl.semaphore_wait(barrier, len(greeted))
 
     def part_of(p, chunk):
@@ -255,25 +257,26 @@
         return pltpu.make_async_remote_copy(
             src_ref=time_out.at[w, d, part_of(p, TIME_CHUNK)], dst_ref=time_in.at[w, d, part_of(p, TIME_CHUNK)],
             send_sem=send_sem.at[1], recv_sem=time_sem.at[lax.rem(w, 2), d, p],
-            device_id=peer("ta", (-1, 1)[d]), device_id_type=MESH,
+            device_id=peer("ta", 2 * d - 1), device_id_type=MESH,
         )
 
     def load_field(ref, p):
         return unflat([ref[p, i] for i in range(24)], 4)
 
     def send_time(f, w, p, par, held=False):
-        def start(d):
-            if held:
-                pl.when(p < PAIRS - 1)(lambda: time_copy(w, d, p).start())
-            else:
-                time_copy(w, d, p).start()
-
         for i, v in enumerate(flat(project(f, 3, -par))):
             time_out[w, 0, p, i] = v
-        start(0)
         for i, v in enumerate(flat(link_times(link, 3, project(f, 3, par), True))):
             time_out[w, 1, p, i] = v
-        start(1)
+        if held:
+            pl.when(p < PAIRS - 1)(lambda: start_time(w, p))
+        else:
+            start_time(w, p)
+
+    def start_time(w, p):
+        last = jnp.where(me["ta"] == n_of["ta"] - 1, 1, 0)
+        for d in (last, 1 - last):
+            time_copy(w, d, p).start()
 
     def send_edges(f, w, p, par):
         for kind, mu in ((0, 1), (1, 2)):
@@ -434,73 +437,65 @@
 
             lax.fori_loop(0, min(2 * deep + 1, n_gz), body, 0)
 
-    def paired(colours):
-        out = []
-        for part in range(2):
-            for q in range(2):
-                for a in range(3):
-                    i = part * 3 + a
-                    up, down = colours[2 * q][i], colours[1 + q][i]
-                    out.append(jnp.where(sh.low, up, pltpu.roll(down, 4, 0)))
-        return out
+    def both_halves(items):
+        return [jnp.where(sh.low, v, pltpu.roll(v, 4, 0)) for v in items]
 
     def start_right(items):
-        for i, v in enumerate(items):
-            smt_out[0, i] = v
-        smt_copy(0).start()
-        for i, v in enumerate(flat(link_times(link, 3, unflat(items, 2), True))):
-            smt_out[1, i] = v
-        smt_copy(1).start()
-
-    def local_right(items):
-        done = [colour_hops(NSMEAR % 2, own // 2, me["gz"], c)[1] for c in range(3)]
-        for mu in range(3):
-            take(mu, items, *(paired([parts[mu][side] for parts in done]) for side in range(2)))
+        carried_on = flat(link_times(link, 3, unflat(items, 1), True))
+        for d, values in enumerate((items, carried_on)):
+            for a in range(3):
+                smt_out[d, a] = jnp.where(sh.low, values[a], values[3 + a])
+            smt_copy(d).start()
+
+    def from_time(d):
+        smt_copy(d).wait_recv()
+        got = [smt_in[d, a] for a in range(3)]
+        turned = [pltpu.roll(v, 4, 0) for v in got]
+        real = [jnp.where(sh.low, v, t) for v, t in zip(got, turned)]
+        return real + [jnp.where(sh.low, t, v) for v, t in zip(got, turned)]
 
     def take(mu, items, ahead, behind):
-        for i in range(12):
+        for i in range(6):
             hops[mu, i] = HOP * (behind[i] - ahead[i])
             part = HOP * (ahead[i] + behind[i])
             hops[4, i] = items[i] - part if mu == 0 else hops[4, i] - part
 
+    def local_right(items):
+        parts = colour_hops(NSMEAR % 2, own // 2, me["gz"], 0)[1]
+        for mu in range(3):
+            take(mu, items, *(both_halves(side) for side in parts[mu]))
+
     def finish_right():
-        smt_copy(0).wait_recv()
-        got = unflat([smt_in[0, i] for i in range(12)], 2)
-        ahead = flat(link_times(link, 3, got, False))
-        smt_copy(1).wait_recv()
-        take(3, None, ahead, [smt_in[1, i] for i in range(12)])
+        take(3, None, flat(link_times(link, 3, unflat(from_time(0), 1), False)), from_time(1))
         zero = jnp.zeros((8, 128), jnp.float32)
 
-        def pick(which, q, a):
-            return hops[which, q * 3 + a], hops[which, 6 + q * 3 + a]
-
-        def block(s2, s, q, a):
+        def pick(which, a):
+            return hops[which, a], hops[which, 3 + a]
+
+        def block(s2, s, a):
             if s2 == s:
-                return pick(4, q, a)
+                return pick(4, a)
             if s2 // 2 == s // 2:
                 return (zero, zero)
-            out = None
+            out = (zero, zero)
             for mu in range(4):
                 for row in range(2):
                     column, coef = E_ROWS[mu][row]
                     if s2 < 2 and row == s2 and column == s - 2:
-                        out = add_term(out or (zero, zero), coef, pick(mu, q, a))
+                        out = add_term(out, coef, pick(mu, a))
                     if s2 >= 2 and column == s2 - 2 and row == s:
-                        out = add_term(out or (zero, zero), complex(coef).conjugate(), pick(mu, q, a))
+                        out = add_term(out, complex(coef).conjugate(), pick(mu, a))
             return out
 
-        for s2 in range(4):
-            for a in range(3):
-                column = [block(s2, s, 0, a) for s in range(4)]
-                lone = [block(s2, s, 1, a) for s in range(4)]
-                for part in range(2):
-                    i = part * 12 + s2 * 3 + a
-                    for s in range(4):
-                        right[s, i] = column[s][part]
-                    right[4, i] = jnp.where(sh.low, lone[0][part], lone[1][part])
-                    right[5, i] = jnp.where(sh.low, lone[2][part], lone[3][part])
+        for h in range(2):
+            for s2 in range(4):
+                for a in range(3):
+                    up, down = (block(s2, 2 * h + k, a) for k in range(2))
+                    for part in range(2):
+                        right[h, part * 12 + s2 * 3 + a] = jnp.where(sh.low, up[part], down[part])
 
     def first_time(p, _):
+        load_guess(p, 0)
         send_time(load_field(guess, p), 0, p, 1)
         return _
 
@@ -511,8 +506,9 @@
     def give(ref, p, out):
         first, second_rhs = rhs_of(p)
         for i, v in enumerate(out):
-            ref[first, i] = v[0:4]
-            ref[second_rhs, i] = v[4:8]
+            place = pl.ds(4 * (i % 2), 4)
+            ref[first, i // 2, place] = v[0:4]
+            ref[second_rhs, i // 2, place] = v[4:8]
 
     def second(p, _):
         out = receive_body(guess, 0, p, 1)
@@ -520,6 +516,26 @@
             field_a[p, i] = v
         send_time(unflat(out, 4), 1, p, -1)
         send_edges(unflat(out, 4), 1, p, -1)
+        return _
+
+    def second_late(p, _):
+        spin = 2 * lax.rem(p, 2) + jnp.where(sh.low, 0, 1)
+        out = receive_body(guess, 0, p, 1)
+        for part in range(2):
+            for s2 in range(4):
+                for a in range(3):
+                    i = part * 12 + s2 * 3 + a
+                    source = jnp.where(spin == s2, sources[p // 2, part * 3 + a], 0.0)
+                    out[i] = out[i] - source
+        for i, v in enumerate(out):
+            field_a[p, i] = v
+        send_time(unflat(out, 4), 1, p, -1)
+        send_edges(unflat(out, 4), 1, p, -1)
+        return _
+
+    def no_right(p, _):
+        for i in range(24):
+            right[p, i] = jnp.zeros((8, 128), jnp.float32)
         return _
 
     def third(p, _):
@@ -539,20 +555,23 @@
 
     send_blocks()
     run(first_time, 0, PAIRS)
+    double_links(0, 54)
     run(first_edges, 0, PAIRS)
     interior(guess, 1)
     pass_blocks()
     run(second, 0, 2)
     await_blocks()
     lax.fori_loop(0, n_gz, widen, 0)
-    smear_steps(0, 3)
-    run(second, 2, 3)
-    smear_steps(3, NSMEAR)
-    items = paired([colour(smear, NSMEAR % 2, own // 2, me["gz"], c) for c in range(3)])
+    smear_steps(0, NSMEAR)
+    for c in range(3):
+        for i, v in enumerate(both_halves(colour(smear, NSMEAR % 2, own // 2, me["gz"], c))):
+            sources[c, i] = v
+    items = [sources[0, i] for i in range(6)]
     start_right(items)
-    run(second, 3, PAIRS)
+    run(second_late, 2, PAIRS)
     local_right(items)
     interior(field_a, -1)
+    run(no_right, 2, PAIRS)
     finish_right()
 
     run(third, 0, PAIRS)
@@ -594,8 +613,7 @@
         if stage == 0:
             interior(field_b, -1)
         if stage == 2:
-            for d in range(2):
-                time_copy(3, d, PAIRS - 1).start()
+            start_time(3, PAIRS - 1)
             run(normal_of, 0, PAIRS - 1)
         for copy, place in copies:
             copy.wait_recv()
@@ -609,7 +627,8 @@
     run(normal_of, PAIRS - 1, PAIRS)
     for p in range(PAIRS):
         length = jnp.sum(jnp.where(sh.lane == p, steps, 0.0), axis=1, keepdims=True)
-        first, second_rhs = (3 * p, 3 * p + 1) if p < 4 else (6 * p - 22, 6 * p - 19)
+        first = 6 * (p % 2) + p // 2
+        second_rhs = first + 3
         length_ref[first : first + 1] = jnp.broadcast_to(length[0:1], (1, 128))
         length_ref[second_rhs : second_rhs + 1] = jnp.broadcast_to(length[4:5], (1, 128))
 
@@ -633,7 +652,7 @@
     tile = (8, lanes)
     vm = lambda *shape: pltpu.VMEM(shape + tile, f32)
     dma = lambda *shape: pltpu.SemaphoreType.DMA(shape)
-    out = jax.ShapeDtypeStruct((12, 24, rows, lanes), f32)
+    out = jax.ShapeDtypeStruct((12, 12, 2 * rows, lanes), f32)
     search, normal, length = pl.pallas_call(
         functools.partial(kernel, sizes),
         out_shape=(out, out, jax.ShapeDtypeStruct((12, lanes), f32)),
@@ -650,8 +669,8 @@
             vm(72), vm(PAIRS, 24), vm(PAIRS, 24), vm(PAIRS, 24), vm(PAIRS, 24), vm(PAIRS, 24),
             vm(PAIRS, 24), vm(2, PAIRS, 12),
             vm(4, 4, PAIRS, 3), vm(4, 4, PAIRS, 3), vm(4, 2, PAIRS, 12), vm(4, 2, PAIRS, 12),
-            vm(2, 12), vm(2, 12),
-            vm(3), vm(copies), vm(2 * PAIRS), vm(5, 12),
+            vm(2, 3), vm(2, 3),
+            vm(3), vm(copies), vm(2 * PAIRS), vm(5, 6), vm(3, 6),
             dma(4), dma(2, 4, PAIRS // EDGE_CHUNK), dma(2, 2, PAIRS), dma(reach * n_gz), dma(2), dma(copies), dma(5),
         ],
         compiler_params=pltpu.CompilerParams(

time: 64.4 us -> 62.1 us (0.964)
  Pallas kernels: 62.3 us -> 60.2 us
    pallas_call x1, Pallas kernels: 62.3 us -> 60.2 us  [on_device(): pl.pallas_call(functools.partial(kernel, sizes), out_shape=(out, out, jax...]
where the time goes in v3:
time: 62.1 us; the launch traced here: 62 us
  Pallas kernels  60.2 us (97%)
  other arithmetic  1.15 us (2%)
  between operations  0.65 us (1%)
    pallas_call x1, Pallas kernels, on_device(): pl.pallas_call(functools.partial(kernel, sizes), out_shape=(out, out, jax...  60.2 us

profile of v3, /device:TPU:0, one launch (start us, length us, event | category | flops | bytes accessed | tf_op | source)
XLA Modules:
  0.0 62.0 jit_solution(9252260121117696261)
XLA Ops:
  0.6 0.0 copy-start
  0.6 60.2 %shard_map.50 = (f32[12,12,8,128]{3,2,1,0:T(8,128)S(1)}, f32[12,12,8,128]{3,2,1,0:T(8,128)S(1)}, f32[12,128]{1,0:T(8,128)S(1)}) custom-call(s32[4]{0:T(128)} %bitcast.15, f32[72,4,128]{2,1,0:T(4,128)} %bitcast.14, f32[12,24,4,128]{3,2,1,0:T(4,128)} %bitcast.10), custom_call_target="tpu_custom_call" | custom-call | tf_op jit(solution)/shard_map/pallas_call | solution.py:656
  60.8 0.0 copy-done
  60.8 1.1 %multiply_subtract_fusion = (f32[12,12,8,128]{3,2,1,0:T(8,128)}, f32[12,12,8,128]{3,2,1,0:T(8,128)}) fusion(f32[12,12,8,128]{3,2,1,0:T(8,128)S(1)} %get-tuple-element.6, f32[12,12,8,128]{3,2,1,0:T(8,128)S(1)} %get-tuple-element.7, f32[12,128]{1,0:T(8,128)S(1)} %get-tuple-element.5, f32[12,12,8,128]{3,2,1,0:T(8,128)S(1)} %bitcast.11), kind=kLoop, calls=%fused_computation | loop fusion | flops 589824 | bytes 2955264 | tf_op jit(solution)/shard_map/sub | solution.py:687
Async XLA Ops:
  0.6 60.2 %copy-start = (f32[12,2,4,3,1,4,128]{6,5,4,3,2,1,0:T(4,128)S(1)}, f32[12,2,4,3,1,4,128]{6,5,4,3,2,1,0:T(4,128)}, u32[]{:S(2)}) copy-start(f32[12,2,4,3,1,4,128]{6,5,4,3,2,1,0:T(4,128)} %param.4) | copy-start | bytes 1769476

commit v4 on v3

--- a/solution.py
+++ b/solution.py
@@ -236,29 +236,29 @@
             def _():
                 make(w, d, p - (chunk - 1)).start()
 
-    def await_first(make, w, p, chunk, dirs):
-        def wait():
-            for d in dirs:
-                make(w, d, p).wait_recv()
-        if chunk == 1:
-            wait()
-        else:
-            pl.when(lax.rem(p, chunk) == 0)(wait)
-
     def edge_copy(w, d, p):
-        axis, step = (("xy", -1), ("xy", 1), ("gz", -1), ("gz", 1))[d]
+        axis, step = (("xy", -1), ("xy", 1), ("gz", -1), ("gz", 1))[0 if isinstance(d, slice) else d]
         return pltpu.make_async_remote_copy(
             src_ref=edge_out.at[w, d, part_of(p, EDGE_CHUNK)], dst_ref=edge_in.at[w, d, part_of(p, EDGE_CHUNK)],
-            send_sem=send_sem.at[0], recv_sem=edge_sem.at[lax.rem(w, 2), d, p // EDGE_CHUNK],
+            send_sem=send_sem.at[0], recv_sem=edge_sem.at[lax.rem(w, 2), p // EDGE_CHUNK],
             device_id=peer(axis, step), device_id_type=MESH,
         )
 
     def time_copy(w, d, p):
         return pltpu.make_async_remote_copy(
             src_ref=time_out.at[w, d, part_of(p, TIME_CHUNK)], dst_ref=time_in.at[w, d, part_of(p, TIME_CHUNK)],
-            send_sem=send_sem.at[1], recv_sem=time_sem.at[lax.rem(w, 2), d, p],
-            device_id=peer("ta", 2 * d - 1), device_id_type=MESH,
+            send_sem=send_sem.at[1], recv_sem=time_sem.at[lax.rem(w, 2), p],
+            device_id=peer("ta", 1 if isinstance(d, slice) else 2 * d - 1), device_id_type=MESH,
         )
+
+    def await_edges(w, p):
+        def wait():
+            edge_copy(w, slice(None), p).wait_recv()
+
+        pl.when(lax.rem(p, EDGE_CHUNK) == 0)(wait)
+
+    def await_time(w, p):
+        time_copy(w, slice(None), p).wait_recv()
 
     def load_field(ref, p):
         return unflat([ref[p, i] for i in range(24)], 4)
@@ -305,8 +305,8 @@
         lax.fori_loop(first, end, body, 0)
 
     def receive_body(src, w, p, par):
-        await_first(edge_copy, w, p, EDGE_CHUNK, range(4))
-        await_first(time_copy, w, p, TIME_CHUNK, range(2))
+        await_edges(w, p)
+        await_time(w, p)
         f = load_field(src, p)
         total = load_field(acc, p)
         for kind, mu in ((0, 1), (1, 2)):
@@ -350,20 +350,15 @@
     def smt_copy(d):
         return pltpu.make_async_remote_copy(
             src_ref=smt_out.at[d], dst_ref=smt_in.at[d],
-            send_sem=send_sem.at[3], recv_sem=smt_sem.at[d],
-            device_id=peer("ta", (-1, 1)[d]), device_id_type=MESH,
+            send_sem=send_sem.at[3], recv_sem=smt_sem.at[0],
+            device_id=peer("ta", 1 if isinstance(d, slice) else 2 * d - 1), device_id_type=MESH,
         )
 
     def widen(z, _):
-        zero = jnp.zeros((8, 128), jnp.float32)
         for g in range(groups):
             for i in range(55):
                 wide[g, z, i, 0:4] = blocks[2 * g * n_gz + z, i]
                 wide[g, z, i, 4:8] = blocks[(2 * g + 1) * n_gz + z, i]
-            for c in range(3):
-                for i in range(6):
-                    smear[0, g, z, c * 6 + i] = wide[g, z, 0] if i == c else zero
-            carry_hops(0, g, z)
         return _
 
     def links_of(g, z):
@@ -416,6 +411,45 @@
         ))
         return items, out
 
+    def from_points(g, z):
+        point = wide[g, z, 0]
+        return [
+            [[(wide[g, z, 1 + mu * 18 + c * 3 + a] * point, wide[g, z, 10 + mu * 18 + c * 3 + a] * -point)
+              for a in range(3)] for c in range(3)]
+            for mu in range(3)
+        ]
+
+    def first_step(k, _):
+        z = lax.rem(me["gz"] + k, n_gz)
+        for g in range(groups):
+            point = wide[g, z, 0]
+            after, before = lax.rem(z + 1, n_gz), lax.rem(z + n_gz - 1, n_gz)
+            up = None if groups == 1 else wide[(g + 1) % groups, z, 0]
+            ahead = [
+                sh.along_x([point], True)[0], beyond([point], [up], 0, True)[0],
+                beyond([point], [wide[g, after, 0]], 1, True)[0],
+            ]
+            back = from_points(g, z)
+            below = None if groups == 1 else from_points((g - 1) % groups, z)
+            beside = from_points(g, before)
+            for c in range(3):
+                sides = [
+                    sh.along_x(flat([back[0][c]]), False),
+                    beyond(flat([back[1][c]]), [None] * 6 if groups == 1 else flat([below[1][c]]), 0, False),
+                    beyond(flat([back[2][c]]), flat([beside[2][c]]), 1, False),
+                ]
+                for part in range(2):
+                    for a in range(3):
+                        i = part * 3 + a
+                        total = None
+                        for mu in range(3):
+                            term = wide[g, z, 1 + mu * 18 + part * 9 + a * 3 + c] * ahead[mu] + sides[mu][i]
+                            total = term if total is None else total + term
+                        value = 0.25 * total if i != c else point + 0.25 * total
+                        smear[1, g, z, c * 6 + i] = value * 0.5
+            carry_hops(1, g, z)
+        return _
+
     def smear_steps(first, end):
         for step in range(first, end):
             now, then = step % 2, (step + 1) % 2
@@ -448,7 +482,6 @@
             smt_copy(d).start()
 
     def from_time(d):
-        smt_copy(d).wait_recv()
         got = [smt_in[d, a] for a in range(3)]
         turned = [pltpu.roll(v, 4, 0) for v in got]
         real = [jnp.where(sh.low, v, t) for v, t in zip(got, turned)]
@@ -466,6 +499,7 @@
             take(mu, items, *(both_halves(side) for side in parts[mu]))
 
     def finish_right():
+        smt_copy(slice(None)).wait_recv()
         take(3, None, flat(link_times(link, 3, unflat(from_time(0), 1), False)), from_time(1))
         zero = jnp.zeros((8, 128), jnp.float32)
 
@@ -559,10 +593,13 @@
     run(first_edges, 0, PAIRS)
     interior(guess, 1)
     pass_blocks()
-    run(second, 0, 2)
+    run(second, 0, 1)
     await_blocks()
     lax.fori_loop(0, n_gz, widen, 0)
-    smear_steps(0, NSMEAR)
+    lax.fori_loop(0, n_gz, first_step, 0)
+    smear_steps(1, 3)
+    run(second, 1, 2)
+    smear_steps(3, NSMEAR)
     for c in range(3):
         for i, v in enumerate(both_halves(colour(smear, NSMEAR % 2, own // 2, me["gz"], c))):
             sources[c, i] = v
@@ -600,37 +637,44 @@
     slot = 0
     for stage, axis in enumerate(AXES):
         red_out[stage] = mine
-        copies = []
-        for k in range(1, n_of[axis]):
-            copy = pltpu.make_async_remote_copy(
-                src_ref=red_out.at[stage], dst_ref=red_in.at[slot],
-                send_sem=send_sem.at[4], recv_sem=red_sem.at[slot],
+        others = n_of[axis] - 1
+
+        def sum_copy(k, place):
+            return pltpu.make_async_remote_copy(
+                src_ref=red_out.at[stage], dst_ref=red_in.at[place],
+                send_sem=send_sem.at[4], recv_sem=red_sem.at[stage],
                 device_id=peer(axis, k), device_id_type=MESH,
             )
-            copy.start()
-            copies.append((copy, slot))
-            slot += 1
+
+        for k in range(1, others + 1):
+            sum_copy(k, slot + k - 1).start()
         if stage == 0:
             interior(field_b, -1)
         if stage == 2:
             start_time(3, PAIRS - 1)
             run(normal_of, 0, PAIRS - 1)
-        for copy, place in copies:
-            copy.wait_recv()
-            mine = mine + red_in[place]
+        landed = red_in.at[pl.ds(slot, others)]
+        pltpu.make_async_remote_copy(
+            src_ref=landed, dst_ref=landed, send_sem=send_sem.at[4], recv_sem=red_sem.at[stage],
+            device_id=peer(axis, 1), device_id_type=MESH,
+        ).wait_recv()
+        for k in range(others):
+            mine = mine + red_in[slot + k]
+        slot += others
     top = jnp.sum(mine[0:4], axis=0, keepdims=True)
     bottom = jnp.sum(mine[4:8], axis=0, keepdims=True)
     both = jnp.where(sh.low, top, bottom)
     curvature = pltpu.roll(both, 128 - PAIRS, 1)
     steps = both / jnp.where(sh.lane < PAIRS, curvature, 1.0)
 
-    run(normal_of, PAIRS - 1, PAIRS)
     for p in range(PAIRS):
         length = jnp.sum(jnp.where(sh.lane == p, steps, 0.0), axis=1, keepdims=True)
         first = 6 * (p % 2) + p // 2
         second_rhs = first + 3
         length_ref[first : first + 1] = jnp.broadcast_to(length[0:1], (1, 128))
         length_ref[second_rhs : second_rhs + 1] = jnp.broadcast_to(length[4:5], (1, 128))
+
+    run(normal_of, PAIRS - 1, PAIRS)
 
     passed = blocks.at[pl.ds(0, reach * n_gz - 1)]
     for k, (sent, landed) in enumerate((
@@ -671,7 +715,7 @@
             vm(4, 4, PAIRS, 3), vm(4, 4, PAIRS, 3), vm(4, 2, PAIRS, 12), vm(4, 2, PAIRS, 12),
             vm(2, 3), vm(2, 3),
             vm(3), vm(copies), vm(2 * PAIRS), vm(5, 6), vm(3, 6),
-            dma(4), dma(2, 4, PAIRS // EDGE_CHUNK), dma(2, 2, PAIRS), dma(reach * n_gz), dma(2), dma(copies), dma(5),
+            dma(4), dma(2, PAIRS // EDGE_CHUNK), dma(2, PAIRS), dma(reach * n_gz), dma(1), dma(3), dma(5),
         ],
         compiler_params=pltpu.CompilerParams(
             collective_id=0, has_side_effects=True, vmem_limit_bytes=48 * 1024 * 1024

time: 62.1 us -> 61.9 us (level)
  no operation moved by 1% of the time
where the time goes in v4:
time: 61.9 us; the launch traced here: 61.7 us
  Pallas kernels  59.9 us (97%)
  other arithmetic  1.15 us (2%)
  between operations  0.65 us (1%)
    pallas_call x1, Pallas kernels, on_device(): pl.pallas_call(functools.partial(kernel, sizes), out_shape=(out, out, jax...  59.9 us

profile of v4, /device:TPU:0, one launch (start us, length us, event | category | flops | bytes accessed | tf_op | source)
XLA Modules:
  0.0 61.7 jit_solution(7734453844135478759)
XLA Ops:
  0.6 0.0 copy-start
  0.6 59.9 %shard_map.50 = (f32[12,12,8,128]{3,2,1,0:T(8,128)S(1)}, f32[12,12,8,128]{3,2,1,0:T(8,128)S(1)}, f32[12,128]{1,0:T(8,128)S(1)}) custom-call(s32[4]{0:T(128)} %bitcast.15, f32[72,4,128]{2,1,0:T(4,128)} %bitcast.14, f32[12,24,4,128]{3,2,1,0:T(4,128)} %bitcast.10), custom_call_target="tpu_custom_call" | custom-call | tf_op jit(solution)/shard_map/pallas_call | solution.py:700
  60.6 0.0 copy-done
  60.6 1.1 %multiply_subtract_fusion = (f32[12,12,8,128]{3,2,1,0:T(8,128)}, f32[12,12,8,128]{3,2,1,0:T(8,128)}) fusion(f32[12,12,8,128]{3,2,1,0:T(8,128)S(1)} %get-tuple-element.6, f32[12,12,8,128]{3,2,1,0:T(8,128)S(1)} %get-tuple-element.7, f32[12,128]{1,0:T(8,128)S(1)} %get-tuple-element.5, f32[12,12,8,128]{3,2,1,0:T(8,128)S(1)} %bitcast.11), kind=kLoop, calls=%fused_computation | loop fusion | flops 589824 | bytes 2955264 | tf_op jit(solution)/shard_map/sub | solution.py:731
Async XLA Ops:
  0.6 59.9 %copy-start = (f32[12,2,4,3,1,4,128]{6,5,4,3,2,1,0:T(4,128)S(1)}, f32[12,2,4,3,1,4,128]{6,5,4,3,2,1,0:T(4,128)}, u32[]{:S(2)}) copy-start(f32[12,2,4,3,1,4,128]{6,5,4,3,2,1,0:T(4,128)} %param.4) | copy-start | bytes 1769476

commit v5 on v4

--- a/solution.py
+++ b/solution.py
@@ -263,13 +263,16 @@
     def load_field(ref, p):
         return unflat([ref[p, i] for i in range(24)], 4)
 
+    first_core = lax.rem(me["gz"], 2) == 0
+    other_core = lax.rem(me["gz"], 2) == 1
+
     def send_time(f, w, p, par, held=False):
         for i, v in enumerate(flat(project(f, 3, -par))):
             time_out[w, 0, p, i] = v
         for i, v in enumerate(flat(link_times(link, 3, project(f, 3, par), True))):
             time_out[w, 1, p, i] = v
         if held:
-            pl.when(p < PAIRS - 1)(lambda: start_time(w, p))
+            pl.when((p < PAIRS - 2) | ((p < PAIRS - 1) & first_core))(lambda: start_time(w, p))
         else:
             start_time(w, p)
 
@@ -651,8 +654,12 @@
         if stage == 0:
             interior(field_b, -1)
         if stage == 2:
-            start_time(3, PAIRS - 1)
-            run(normal_of, 0, PAIRS - 1)
+            pl.when(first_core)(lambda: start_time(3, PAIRS - 1))
+            run(normal_of, 0, PAIRS - 3)
+            pl.when(other_core)(lambda: start_time(3, PAIRS - 2))
+            run(normal_of, PAIRS - 3, PAIRS - 2)
+            pl.when(other_core)(lambda: start_time(3, PAIRS - 1))
+            run(normal_of, PAIRS - 2, PAIRS - 1)
         landed = red_in.at[pl.ds(slot, others)]
         pltpu.make_async_remote_copy(
             src_ref=landed, dst_ref=landed, send_sem=send_sem.at[4], recv_sem=red_sem.at[stage],

time: 61.9 us -> 61.3 us (level)
  no operation moved by 1% of the time
where the time goes in v5:
time: 61.3 us; the launch traced here: 61.1 us
  Pallas kernels  59.3 us (97%)
  other arithmetic  1.15 us (2%)
  between operations  0.65 us (1%)
    pallas_call x1, Pallas kernels, on_device(): pl.pallas_call(functools.partial(kernel, sizes), out_shape=(out, out, jax...  59.3 us

profile of v5, /device:TPU:0, one launch (start us, length us, event | category | flops | bytes accessed | tf_op | source)
XLA Modules:
  0.0 61.1 jit_solution(11401111597537657051)
XLA Ops:
  0.6 0.0 copy-start
  0.6 59.3 %shard_map.50 = (f32[12,12,8,128]{3,2,1,0:T(8,128)S(1)}, f32[12,12,8,128]{3,2,1,0:T(8,128)S(1)}, f32[12,128]{1,0:T(8,128)S(1)}) custom-call(s32[4]{0:T(128)} %bitcast.15, f32[72,4,128]{2,1,0:T(4,128)} %bitcast.14, f32[12,24,4,128]{3,2,1,0:T(4,128)} %bitcast.10), custom_call_target="tpu_custom_call" | custom-call | tf_op jit(solution)/shard_map/pallas_call | solution.py:707
  60.0 0.0 copy-done
  60.0 1.1 %multiply_subtract_fusion = (f32[12,12,8,128]{3,2,1,0:T(8,128)}, f32[12,12,8,128]{3,2,1,0:T(8,128)}) fusion(f32[12,12,8,128]{3,2,1,0:T(8,128)S(1)} %get-tuple-element.6, f32[12,12,8,128]{3,2,1,0:T(8,128)S(1)} %get-tuple-element.7, f32[12,128]{1,0:T(8,128)S(1)} %get-tuple-element.5, f32[12,12,8,128]{3,2,1,0:T(8,128)S(1)} %bitcast.11), kind=kLoop, calls=%fused_computation | loop fusion | flops 589824 | bytes 2955264 | tf_op jit(solution)/shard_map/sub | solution.py:738
Async XLA Ops:
  0.6 59.4 %copy-start = (f32[12,2,4,3,1,4,128]{6,5,4,3,2,1,0:T(4,128)S(1)}, f32[12,2,4,3,1,4,128]{6,5,4,3,2,1,0:T(4,128)}, u32[]{:S(2)}) copy-start(f32[12,2,4,3,1,4,128]{6,5,4,3,2,1,0:T(4,128)} %param.4) | copy-start | bytes 1769476

commit v6 on v5

--- a/solution.py
+++ b/solution.py
@@ -181,7 +181,7 @@
         }
 
     shifts = sorted({(slot - own) % n_of["xy"] for slot in range(reach)} | {(own - slot) % n_of["xy"] for slot in range(reach)})
-    greeted = [across(y, z) for y in shifts for z in range(n_gz) if (y, z) != (0, 0)]
+    greeted = [across(y, z) for y in shifts for z in range(0, n_gz, 1 if y == 0 else 2) if (y, z) != (0, 0)]
     greeted += [peer("xy", y) for y in range(1, n_of["xy"]) if y not in shifts]
     greeted += [peer("ta", t) for t in range(1, n_of["ta"])]
     barrier = pltpu.get_barrier_semaphore()

time: 61.3 us -> 60.6 us (0.989)
  Pallas kernels: 59.3 us -> 58.3 us
    pallas_call x1, Pallas kernels: 59.3 us -> 58.3 us  [on_device(): pl.pallas_call(functools.partial(kernel, sizes), out_shape=(out, out, jax...]
where the time goes in v6:
time: 60.6 us; the launch traced here: 60.1 us
  Pallas kernels  58.3 us (96%)
  other arithmetic  1.15 us (2%)
  between operations  0.65 us (1%)
    pallas_call x1, Pallas kernels, on_device(): pl.pallas_call(functools.partial(kernel, sizes), out_shape=(out, out, jax...  58.3 us

profile of v6, /device:TPU:0, one launch (start us, length us, event | category | flops | bytes accessed | tf_op | source)
XLA Modules:
  0.0 60.1 jit_solution(17498050629874146812)
XLA Ops:
  0.6 0.0 copy-start
  0.6 58.3 %shard_map.50 = (f32[12,12,8,128]{3,2,1,0:T(8,128)S(1)}, f32[12,12,8,128]{3,2,1,0:T(8,128)S(1)}, f32[12,128]{1,0:T(8,128)S(1)}) custom-call(s32[4]{0:T(128)} %bitcast.15, f32[72,4,128]{2,1,0:T(4,128)} %bitcast.14, f32[12,24,4,128]{3,2,1,0:T(4,128)} %bitcast.10), custom_call_target="tpu_custom_call" | custom-call | tf_op jit(solution)/shard_map/pallas_call | solution.py:707
  58.9 0.0 copy-done
  58.9 1.1 %multiply_subtract_fusion = (f32[12,12,8,128]{3,2,1,0:T(8,128)}, f32[12,12,8,128]{3,2,1,0:T(8,128)}) fusion(f32[12,12,8,128]{3,2,1,0:T(8,128)S(1)} %get-tuple-element.6, f32[12,12,8,128]{3,2,1,0:T(8,128)S(1)} %get-tuple-element.7, f32[12,128]{1,0:T(8,128)S(1)} %get-tuple-element.5, f32[12,12,8,128]{3,2,1,0:T(8,128)S(1)} %bitcast.11), kind=kLoop, calls=%fused_computation | loop fusion | flops 589824 | bytes 2955264 | tf_op jit(solution)/shard_map/sub | solution.py:738
Async XLA Ops:
  0.6 58.3 %copy-start = (f32[12,2,4,3,1,4,128]{6,5,4,3,2,1,0:T(4,128)S(1)}, f32[12,2,4,3,1,4,128]{6,5,4,3,2,1,0:T(4,128)}, u32[]{:S(2)}) copy-start(f32[12,2,4,3,1,4,128]{6,5,4,3,2,1,0:T(4,128)} %param.4) | copy-start | bytes 1769476
